TPU v7x, 32 devices: a whole 2x2x4 slice. The times are simulated.
32 devices in a mesh: ctx: 4 (over y, x), head: 8 (over z, core).
Axes of the slice: x: 2, y: 2, z: 4, core: 2. Of those that a mesh axis runs over, the one named last changes fastest.
Arguments:
- state: bfloat16 [4096, 2048], P('ctx'), may hold values from -6 to 6
- norm_gain: bfloat16 [2048], replicated, may hold values from 0.5 to 1.5
- w_qkv: bfloat16 [3, 2048, 2048], P(None, None, 'head'), may hold values from -2 to 2
- w_out: bfloat16 [2048, 2048], P('head'), may hold values from -0.125 to 0.125
- probe: bfloat16 [4096, 2048], P('ctx'), may hold values from -6 to 6
- noise: bfloat16 [4096, 2048], P(('ctx', 'head')), may hold values from -6 to 6
- segment_ids: int32 [4096], P('ctx'), may hold values from 0 to 2, never falling along the last dimension, each value on 1 to 3072 neighbouring positions
Outputs:
- new_state: float32 [4096, 2048], P(('ctx', 'head'))
Inputs may be any that keep to these rules, and one draw needn't show every extreme that they name: `segment_ids`: segment numbers never fall along the sequence; a segment holds at most 3072 positions.
All inputs are finite; a program needn't handle non-finite values.
Results may differ from a plain program's by a relative error of at most 0.011.
Values may be sent and summed in bfloat16 or wider, within the bound.
A program may use at most 128 MiB of HBM per device.

v0:
```python
import functools

import jax
import jax.numpy as jnp
from jax import lax
from jax.experimental import pallas as pl
from jax.experimental.pallas import tpu as pltpu
from jax.sharding import PartitionSpec as P

HEAD_DIM = 128
EPSILON = 1e-05
STEP_SIZE = 0.25
NEGATIVE = -1e30
LOG2E = 1.4426950408889634
MESH = pl.DeviceIdType.MESH
VMEM = pl.BlockSpec(memory_space=pltpu.VMEM)
ANY = pl.BlockSpec(memory_space=pl.ANY)
NT = (((1,), (1,)), ((), ()))
TN = (((0,), (0,)), ((), ()))
FORWARD_BLOCKS = (512, 512)
BACKWARD_BLOCKS = (512, 512)


def row_scale(matrix):
    return lax.rsqrt(jnp.mean(matrix * matrix, axis=-1, keepdims=True) + EPSILON)


def dot32(left, right, dims):
    return lax.dot_general(left, right, dims, preferred_element_type=jnp.float32)


def greet(axis, number, me):
    barrier = pltpu.get_barrier_semaphore()
    for step in range(1, number):
        pl.semaphore_signal(
            barrier, inc=1, device_id={axis: lax.rem(me + step, number)}, device_id_type=MESH
        )
    pl.semaphore_wait(barrier, number - 1)


def gather_kernel(
    number, key_ref, value_ref, seg_ref, normed_ref, w_ref, keys, values, segs, query_out, send_sem,
    recv_sem, own_sem,
):
    me = lax.axis_index("ctx")
    rows = key_ref.shape[0]
    greet("ctx", number, me)

    def place(index):
        return pl.ds(pl.multiple_of(index * rows, rows), rows)

    def send(slot, source, target, peer):
        copy = pltpu.make_async_remote_copy(
            src_ref=source,
            dst_ref=target,
            send_sem=send_sem.at[slot],
            recv_sem=recv_sem.at[slot],
            device_id={"ctx": peer},
            device_id_type=MESH,
        )
        copy.start()
        return copy

    mine = place(me)
    copies = []
    for step in range(1, number):
        copies.append(send(step, seg_ref, segs.at[me], lax.rem(me + step, number)))
    relay = number == 4
    if relay:
        low, high = lax.rem(me, 2), me // 2
        across, along = high * 2 + 1 - low, (1 - high) * 2 + low
        key_first = send(number, key_ref, keys.at[mine], across)
        value_first = send(number + 1, value_ref, values.at[mine], along)
        copies.append(send(number + 2, value_ref, values.at[mine], across))
        copies.append(send(number + 3, key_ref, keys.at[mine], along))
    else:
        for step in range(1, number):
            peer = lax.rem(me + step, number)
            copies.append(send(number + 2 * step, key_ref, keys.at[mine], peer))
            copies.append(send(number + 2 * step + 1, value_ref, values.at[mine], peer))
    pairs = ((key_ref, keys.at[mine]), (value_ref, values.at[mine]), (seg_ref, segs.at[me]))
    for index, (source, target) in enumerate(pairs):
        copy = pltpu.make_async_copy(source, target, own_sem.at[index])
        copy.start()
        copies.append(copy)
    tile = min(256, rows)

    def project(piece, _):
        at = pl.ds(pl.multiple_of(piece * tile, tile), tile)
        query_out[at, :] = jnp.dot(
            normed_ref[at, :], w_ref[...], preferred_element_type=jnp.float32
        ).astype(jnp.bfloat16)
        return 0

    lax.fori_loop(0, rows // tile, project, 0)
    if relay:
        key_first.wait()
        copies.append(send(number + 4, keys.at[place(across)], keys.at[place(across)], along))
        value_first.wait()
        copies.append(send(number + 5, values.at[place(along)], values.at[place(along)], across))
    for copy in copies:
        copy.wait()


def gather_keys(number, key_rows, value_rows, segment_ids, normed, w_query):
    rows, width = key_rows.shape
    seg = segment_ids.reshape(-1, 128)
    full = jax.ShapeDtypeStruct((number * rows, width), key_rows.dtype)
    keys, values, segs, queries = pl.pallas_call(
        functools.partial(gather_kernel, number),
        out_shape=(
            full,
            full,
            jax.ShapeDtypeStruct((number,) + seg.shape, seg.dtype),
            jax.ShapeDtypeStruct((rows, width), key_rows.dtype),
        ),
        in_specs=[VMEM] * 5,
        out_specs=(ANY, ANY, ANY, VMEM),
        scratch_shapes=[
            pltpu.SemaphoreType.DMA((3 * number + 6,)),
            pltpu.SemaphoreType.DMA((3 * number + 6,)),
            pltpu.SemaphoreType.DMA((3,)),
        ],
        compiler_params=pltpu.CompilerParams(collective_id=0, has_side_effects=True),
    )(key_rows, value_rows, seg, normed, w_query)
    return keys, values, segs.reshape(-1), queries


def block_ranges(table, index):
    return [table[index, column] for column in range(4)]


def forward_kernel(
    heads, bq, bk, table, query_ref, key_ref, value_ref, start_ref, pos_ref, out_ref, log_ref
):
    factor = HEAD_DIM ** (-0.5) * LOG2E
    blocks = query_ref.shape[0] // bq

    def one_block(index, _):
        low, inner_low, inner_high, high = block_ranges(table, index)
        rows = pl.ds(pl.multiple_of(index * bq, bq), bq)
        start, pos = start_ref[index], pos_ref[index]

        def step(masked, piece, carry):
            keys_at = pl.ds(pl.multiple_of(piece * bk, bk), bk)
            if masked:
                key_pos = piece * bk + lax.broadcasted_iota(jnp.int32, (bk, bq), 0)
                allowed = (key_pos >= start) & (key_pos <= pos)
            result = []
            for head in range(heads):
                top, total, acc = carry[head]
                cols = pl.ds(head * HEAD_DIM, HEAD_DIM)
                scores = dot32(key_ref[keys_at, cols], query_ref[rows, cols], NT)
                if masked:
                    scores = jnp.where(allowed, scores, NEGATIVE)
                new_top = jnp.maximum(top, jnp.max(scores, axis=0, keepdims=True) * factor)
                weights = jnp.exp2(scores * factor - new_top)
                scale = jnp.exp2(top - new_top)
                total = total * scale + jnp.sum(weights, axis=0, keepdims=True)
                acc = acc * scale + dot32(
                    value_ref[keys_at, cols], weights.astype(jnp.bfloat16), TN
                )
                result.append((new_top, total, acc))
            return tuple(result)

        carry = tuple(
            (
                jnp.full((1, bq), NEGATIVE, jnp.float32),
                jnp.zeros((1, bq), jnp.float32),
                jnp.zeros((HEAD_DIM, bq), jnp.float32),
            )
            for _ in range(heads)
        )
        carry = lax.fori_loop(low, inner_low, functools.partial(step, True), carry)
        carry = lax.fori_loop(inner_low, inner_high, functools.partial(step, False), carry)
        carry = lax.fori_loop(inner_high, high, functools.partial(step, True), carry)
        for head in range(heads):
            top, total, acc = carry[head]
            out_ref[rows, pl.ds(head * HEAD_DIM, HEAD_DIM)] = (acc / total).T.astype(jnp.bfloat16)
            log_ref[index, pl.ds(head, 1), :] = top + jnp.log2(total)
        return 0

    lax.fori_loop(0, blocks, one_block, 0)


def backward_kernel(
    heads, bq, bk, table, query_ref, key_ref, value_ref, grad_ref, out_ref, log_ref, start_ref,
    pos_ref, query_out, pair_out, pair_acc,
):
    score_scale = HEAD_DIM ** (-0.5)
    factor = score_scale * LOG2E
    blocks = query_ref.shape[0] // bq
    width = heads * HEAD_DIM
    pair_rows = pair_acc.shape[0]

    def clear(piece, _):
        at = pl.ds(pl.multiple_of(piece * bk, bk), bk)
        pair_acc[at, :] = jnp.zeros((bk, 2 * width), jnp.float32)
        return 0

    lax.fori_loop(0, pair_rows // bk, clear, 0)

    def one_block(index, _):
        low, inner_low, inner_high, high = block_ranges(table, index)
        rows = pl.ds(pl.multiple_of(index * bq, bq), bq)
        start, pos = start_ref[index], pos_ref[index]
        deltas, logs = [], []
        for head in range(heads):
            cols = pl.ds(head * HEAD_DIM, HEAD_DIM)
            product = grad_ref[rows, cols].astype(jnp.float32) * out_ref[rows, cols].astype(
                jnp.float32
            )
            deltas.append(jnp.sum(product.T, axis=0, keepdims=True))
            logs.append(log_ref[index, pl.ds(head, 1), :])

        def step(masked, piece, carry):
            keys_at = pl.ds(pl.multiple_of(piece * bk, bk), bk)
            if masked:
                key_pos = piece * bk + lax.broadcasted_iota(jnp.int32, (bk, bq), 0)
                allowed = (key_pos >= start) & (key_pos <= pos)
            result = []
            for head in range(heads):
                cols = pl.ds(head * HEAD_DIM, HEAD_DIM)
                value_cols = pl.ds(width + head * HEAD_DIM, HEAD_DIM)
                key_block, query_block = key_ref[keys_at, cols], query_ref[rows, cols]
                grad_block = grad_ref[rows, cols]
                scores = dot32(key_block, query_block, NT)
                probabilities = jnp.exp2(scores * factor - logs[head])
                if masked:
                    probabilities = jnp.where(allowed, probabilities, 0.0)
                dprobs = dot32(value_ref[keys_at, cols], grad_block, NT)
                dscores = (probabilities * (dprobs - deltas[head])).astype(jnp.bfloat16)
                pair_acc[keys_at, value_cols] += jnp.dot(
                    probabilities.astype(jnp.bfloat16),
                    grad_block,
                    preferred_element_type=jnp.float32,
                )
                pair_acc[keys_at, cols] += jnp.dot(
                    dscores, query_block, preferred_element_type=jnp.float32
                )
                result.append(carry[head] + dot32(key_block, dscores, TN))
            return tuple(result)

        carry = tuple(jnp.zeros((HEAD_DIM, bq), jnp.float32) for _ in range(heads))
        carry = lax.fori_loop(low, inner_low, functools.partial(step, True), carry)
        carry = lax.fori_loop(inner_low, inner_high, functools.partial(step, False), carry)
        carry = lax.fori_loop(inner_high, high, functools.partial(step, True), carry)
        for head in range(heads):
            query_out[rows, pl.ds(head * HEAD_DIM, HEAD_DIM)] = (
                carry[head].T * score_scale
            ).astype(jnp.bfloat16)
        return 0

    lax.fori_loop(0, blocks, one_block, 0)

    def flush(piece, _):
        at = pl.ds(pl.multiple_of(piece * bk, bk), bk)
        pair_out[at, :width] = (pair_acc[at, :width] * score_scale).astype(jnp.bfloat16)
        pair_out[at, width:] = pair_acc[at, width:].astype(jnp.bfloat16)
        return 0

    lax.fori_loop(0, pair_rows // bk, flush, 0)


def make_table(start, pos, bq, bk):
    starts, places = start.reshape(-1, bq), pos.reshape(-1, bq)
    low = starts[:, 0] // bk
    inner_low = (starts[:, -1] + bk - 1) // bk
    inner_high = jnp.maximum(inner_low, (places[:, 0] + 1) // bk)
    high = places[:, -1] // bk + 1
    return jnp.stack([low, inner_low, inner_high, high], axis=1).astype(jnp.int32)


def middle_kernel(
    number, part_ref, w_any, state_ref, probe_ref, grad_out, readout_out, w_ref, joined, half,
    sending, landing, send_sem, recv_sem, back_send, back_recv, w_sem,
):
    me = lax.axis_index("head")
    width = part_ref.shape[1]
    own = state_ref.shape[0]
    model = state_ref.shape[1]
    w_copy = pltpu.make_async_copy(w_any, w_ref, w_sem)
    w_copy.start()
    greet("head", number, me)
    my_cols = pl.ds(pl.multiple_of(me * width, width), width)
    my_rows = pl.ds(pl.multiple_of(me * own, own), own)
    copies = []
    for step in range(1, number):
        peer = lax.rem(me + step, number)
        copy = pltpu.make_async_remote_copy(
            src_ref=part_ref.at[pl.ds(pl.multiple_of(peer * own, own), own)],
            dst_ref=joined.at[:, my_cols],
            send_sem=send_sem.at[step],
            recv_sem=recv_sem.at[step],
            device_id={"head": peer},
            device_id_type=MESH,
        )
        copy.start()
        copies.append(copy)
    joined[:, my_cols] = part_ref[my_rows, :]
    w_copy.wait()
    for copy in copies:
        copy.wait()

    tile = min(256, model)

    def project(piece, carry):
        squares, products = carry
        cols = pl.ds(pl.multiple_of(piece * tile, tile), tile)
        layer = state_ref[:, cols].astype(jnp.float32) + jnp.dot(
            joined[...], w_ref[:, cols], preferred_element_type=jnp.float32
        )
        readout_out[:, cols] = layer
        squares = squares + jnp.sum(layer * layer, axis=1, keepdims=True)
        products = products + jnp.sum(
            layer * probe_ref[:, cols].astype(jnp.float32), axis=1, keepdims=True
        )
        return squares, products

    zero = jnp.zeros((own, 1), jnp.float32)
    squares, products = lax.fori_loop(0, model // tile, project, (zero, zero))
    scale = lax.rsqrt(squares / model + EPSILON)
    bend = scale**3 * (products / model)

    def finish(piece, _):
        cols = pl.ds(pl.multiple_of(piece * tile, tile), tile)
        readout = scale * probe_ref[:, cols].astype(jnp.float32) - readout_out[:, cols] * bend
        readout_out[:, cols] = readout
        half[:, cols] = readout.astype(jnp.bfloat16)
        return 0

    lax.fori_loop(0, model // tile, finish, 0)
    copies = []
    for step in range(1, number):
        peer = lax.rem(me + step, number)
        sending[step] = dot32(
            half[...], w_ref[pl.ds(pl.multiple_of(peer * width, width), width), :], NT
        ).astype(jnp.bfloat16)
        copy = pltpu.make_async_remote_copy(
            src_ref=sending.at[step],
            dst_ref=landing.at[my_rows],
            send_sem=back_send.at[step],
            recv_sem=back_recv.at[step],
            device_id={"head": peer},
            device_id_type=MESH,
        )
        copy.start()
        copies.append(copy)
    landing[my_rows, :] = dot32(half[...], w_ref[my_cols, :], NT).astype(jnp.bfloat16)
    for copy in copies:
        copy.wait()
    grad_out[...] = landing[...]


def middle(number, part, w_full, state_own, probe_own):
    rows, width = part.shape
    own, model = state_own.shape
    return pl.pallas_call(
        functools.partial(middle_kernel, number),
        out_shape=(
            jax.ShapeDtypeStruct((rows, width), jnp.bfloat16),
            jax.ShapeDtypeStruct((own, model), jnp.float32),
        ),
        in_specs=[VMEM, ANY, VMEM, VMEM],
        out_specs=(VMEM, VMEM),
        scratch_shapes=[
            pltpu.VMEM(w_full.shape, jnp.bfloat16),
            pltpu.VMEM((own, number * width), jnp.bfloat16),
            pltpu.VMEM((own, model), jnp.bfloat16),
            pltpu.VMEM((number, own, width), jnp.bfloat16),
            pltpu.VMEM((rows, width), jnp.bfloat16),
            pltpu.SemaphoreType.DMA((number,)),
            pltpu.SemaphoreType.DMA((number,)),
            pltpu.SemaphoreType.DMA((number,)),
            pltpu.SemaphoreType.DMA((number,)),
            pltpu.SemaphoreType.DMA,
        ],
        compiler_params=pltpu.CompilerParams(
            collective_id=1, has_side_effects=True, vmem_limit_bytes=60 * 2**20
        ),
    )(part, w_full, state_own, probe_own)


def tail_kernel(
    ctx_count, number, pair_any, query_ref, w_ref, sum_out, own_pair, arriving, gathered, terms,
    from_partner, reduced, landing, ctx_send, ctx_recv, p_send, p_recv, z_send, z_recv, own_sem,
):
    ctx, me = lax.axis_index("ctx"), lax.axis_index("head")
    groups = number // 2
    group, core = me // 2, lax.rem(me, 2)
    partner = group * 2 + 1 - core
    rows, width = query_ref.shape
    own, model = sum_out.shape
    chunk = 2 * own
    own_copy = pltpu.make_async_copy(
        pair_any.at[pl.ds(pl.multiple_of(ctx * rows, rows), rows)], own_pair, own_sem
    )
    own_copy.start()
    barrier = pltpu.get_barrier_semaphore()
    peers = [{"ctx": lax.rem(ctx + step, ctx_count)} for step in range(1, ctx_count)]
    peers.append({"head": partner})
    for step in range(1, groups):
        peers.append({"head": lax.rem(group + step, groups) * 2 + core})
    for peer in peers:
        pl.semaphore_signal(barrier, inc=1, device_id=peer, device_id_type=MESH)
    pl.semaphore_wait(barrier, len(peers))

    def chunk_start(order):
        dest = lax.rem(group + order + 1, groups)
        return dest, pl.multiple_of(dest * chunk, chunk)

    def ctx_copy(order, step):
        target = lax.rem(ctx - step + ctx_count, ctx_count)
        _, first = chunk_start(order)
        return pltpu.make_async_remote_copy(
            src_ref=pair_any.at[pl.ds(pl.multiple_of(target * rows + first, chunk), chunk)],
            dst_ref=arriving.at[order, step - 1],
            send_sem=ctx_send.at[order, step],
            recv_sem=ctx_recv.at[order, step],
            device_id={"ctx": target},
            device_id_type=MESH,
        )

    for order in range(groups):
        for step in range(1, ctx_count):

            @pl.when(step <= ctx)
            def _():
                ctx_copy(order, step).start()

    own_copy.wait()
    tile = min(512, model)
    mine = pl.ds(pl.multiple_of(core * own, own), own)
    theirs = pl.ds(pl.multiple_of((1 - core) * own, own), own)
    waiting = []
    for order in range(groups):
        dest, first = chunk_start(order)
        at = pl.ds(first, chunk)
        gathered[...] = own_pair[at, :].astype(jnp.float32)
        for step in range(1, ctx_count):

            @pl.when(ctx + step < ctx_count)
            def _():
                ctx_copy(order, step).wait_recv()
                gathered[...] += arriving[order, step - 1].astype(jnp.float32)

        def multiply(piece, _):
            cols = pl.ds(pl.multiple_of(piece * tile, tile), tile)
            term = dot32(query_ref[at, :], w_ref[0, cols, :], NT)
            term += dot32(gathered[:, :width].astype(jnp.bfloat16), w_ref[1, cols, :], NT)
            term += dot32(gathered[:, width:].astype(jnp.bfloat16), w_ref[2, cols, :], NT)
            terms[order, :, cols] = term.astype(jnp.bfloat16)
            return 0

        lax.fori_loop(0, model // tile, multiply, 0)
        copy = pltpu.make_async_remote_copy(
            src_ref=terms.at[order, theirs],
            dst_ref=from_partner.at[order],
            send_sem=p_send.at[order],
            recv_sem=p_recv.at[order],
            device_id={"head": partner},
            device_id_type=MESH,
        )
        copy.start()
        copy.wait()
        both = terms[order, mine, :].astype(jnp.float32) + from_partner[order].astype(jnp.float32)
        if order < groups - 1:
            reduced[order] = both.astype(jnp.bfloat16)
            copy = pltpu.make_async_remote_copy(
                src_ref=reduced.at[order],
                dst_ref=landing.at[order],
                send_sem=z_send.at[order],
                recv_sem=z_recv.at[order],
                device_id={"head": dest * 2 + core},
                device_id_type=MESH,
            )
            copy.start()
            waiting.append(copy)
        else:
            sum_out[...] = both
    for order, copy in enumerate(waiting):
        copy.wait()
        sum_out[...] += landing[order].astype(jnp.float32)
    for order in range(groups):
        for step in range(1, ctx_count):

            @pl.when(step <= ctx)
            def _():
                ctx_copy(order, step).wait_send()


def tail(ctx_count, number, pair, query_grad, w_qkv):
    rows, width = query_grad.shape
    model = w_qkv.shape[1]
    own, groups = rows // number, number // 2
    half, full = jnp.bfloat16, jnp.float32
    dma = pltpu.SemaphoreType.DMA
    return pl.pallas_call(
        functools.partial(tail_kernel, ctx_count, number),
        out_shape=jax.ShapeDtypeStruct((own, model), full),
        in_specs=[ANY, VMEM, VMEM],
        out_specs=VMEM,
        scratch_shapes=[
            pltpu.VMEM((rows, 2 * width), half),
            pltpu.VMEM((groups, ctx_count - 1, 2 * own, 2 * width), half),
            pltpu.VMEM((2 * own, 2 * width), full),
            pltpu.VMEM((groups, 2 * own, model), half),
            pltpu.VMEM((groups, own, model), half),
            pltpu.VMEM((groups, own, model), half),
            pltpu.VMEM((groups, own, model), half),
            dma((groups, ctx_count)),
            dma((groups, ctx_count)),
            dma((groups,)),
            dma((groups,)),
            dma((groups,)),
            dma((groups,)),
            dma,
        ],
        compiler_params=pltpu.CompilerParams(
            collective_id=2, has_side_effects=True, vmem_limit_bytes=60 * 2**20
        ),
    )(pair, query_grad, w_qkv)


def body(state, norm_gain, w_qkv, w_out, probe, noise, segment_ids):
    local_rows, model_width = state.shape
    width = w_qkv.shape[2]
    local_heads = width // HEAD_DIM
    head_count = lax.axis_size("head")
    ctx_count = lax.axis_size("ctx")
    ctx_index = lax.axis_index("ctx")
    own_rows = local_rows // head_count
    row_start = lax.axis_index("head") * own_rows
    w_full = lax.all_gather(w_out, "head", axis=0, tiled=True)
    state_f = state.astype(jnp.float32)
    gain_full = norm_gain.astype(jnp.float32)
    inverse = row_scale(state_f)
    normed = (state_f * inverse * gain_full).astype(jnp.bfloat16)

    def project(index):
        return jnp.dot(normed, w_qkv[index], preferred_element_type=jnp.float32).astype(
            jnp.bfloat16
        )

    key_rows, value_rows = project(1), project(2)
    keys, values, segs, query_rows = gather_keys(
        ctx_count, key_rows, value_rows, segment_ids, normed, w_qkv[0]
    )
    total_rows = keys.shape[0]
    pos = ctx_index * local_rows + jnp.arange(local_rows, dtype=jnp.int32)
    start = jnp.sum((segs[None, :] < segment_ids[:, None]).astype(jnp.int32), axis=1)
    fq, fk = (min(local_rows, size) for size in FORWARD_BLOCKS)
    gq, gk = (min(local_rows, size) for size in BACKWARD_BLOCKS)
    smem = pl.BlockSpec(memory_space=pltpu.SMEM)
    params = pltpu.CompilerParams(vmem_limit_bytes=60 * 2**20)
    outputs, logs = pl.pallas_call(
        functools.partial(forward_kernel, local_heads, fq, fk),
        out_shape=(
            jax.ShapeDtypeStruct((local_rows, width), jnp.bfloat16),
            jax.ShapeDtypeStruct((local_rows // fq, local_heads, fq), jnp.float32),
        ),
        in_specs=[smem] + [VMEM] * 5,
        out_specs=(VMEM, VMEM),
        compiler_params=params,
        cost_estimate=pl.CostEstimate(
            flops=4 * local_rows * total_rows * width, bytes_accessed=0, transcendentals=0
        ),
    )(
        make_table(start, pos, fq, fk),
        query_rows,
        keys,
        values,
        start.reshape(-1, 1, fq),
        pos.reshape(-1, 1, fq),
    )
    state_half = lax.dynamic_slice_in_dim(state, row_start, own_rows, 0)
    probe_own = lax.dynamic_slice_in_dim(probe, row_start, own_rows, 0)
    state_own = state_half.astype(jnp.float32)
    inverse_own = row_scale(state_own)
    grads_out, readout_own = middle(head_count, outputs, w_full, state_half, probe_own)
    query_grad, pair = pl.pallas_call(
        functools.partial(backward_kernel, local_heads, gq, gk),
        out_shape=(
            jax.ShapeDtypeStruct((local_rows, width), jnp.bfloat16),
            jax.ShapeDtypeStruct((total_rows, 2 * width), jnp.bfloat16),
        ),
        in_specs=[smem] + [VMEM] * 8,
        out_specs=(VMEM, VMEM),
        scratch_shapes=[pltpu.VMEM((total_rows, 2 * width), jnp.float32)],
        compiler_params=params,
        cost_estimate=pl.CostEstimate(
            flops=10 * local_rows * total_rows * width, bytes_accessed=0, transcendentals=0
        ),
    )(
        make_table(start, pos, gq, gk),
        query_rows,
        keys,
        values,
        grads_out,
        outputs,
        logs.reshape(local_rows // fq, local_heads, fq),
        start.reshape(-1, 1, gq),
        pos.reshape(-1, 1, gq),
    )
    normed_grad = tail(ctx_count, head_count, pair, query_grad, w_qkv)
    gain_grad = normed_grad * gain_full
    gradient = (
        readout_own
        + inverse_own * gain_grad
        - state_own * inverse_own**3 * jnp.mean(gain_grad * state_own, axis=-1, keepdims=True)
    )
    return state_own - STEP_SIZE * gradient + jnp.sqrt(2.0 * STEP_SIZE) * noise.astype(jnp.float32)


def solution(mesh):
    placed = (
        P("ctx", None),
        P(),
        P(None, None, "head"),
        P("head", None),
        P("ctx", None),
        P(("ctx", "head"), None),
        P("ctx"),
    )
    return jax.shard_map(
        body, mesh=mesh, in_specs=placed, out_specs=P(("ctx", "head"), None), check_vma=False
    )
```

profile of v0, /device:TPU:11, one launch (start us, length us, event | category | flops | bytes accessed | tf_op | source)
XLA Modules:
  0.0 254.2 jit_solution(6828138583546902247)
XLA Ops:
  6.5 0.0 all-gather.2.cloned.1.call-start
  6.5 0.7 all-gather.2.cloned.1.call-update
  7.3 0.0 copy-start
  7.3 0.8 convert_element_type.26
  8.1 3.3 %fusion = f32[1024]{0:T(1024)S(1)} fusion(bf16[1024,2048]{1,0:T(8,128)(2,1)} %param.7), kind=kLoop, calls=%fused_computation.3 | loop fusion | flops 6290432 | bytes 4198400 | tf_op jit(solution)/shard_map/reduce_sum | solution.py:25
  11.4 0.0 copy-done
  11.4 0.0 copy-start.3
  11.4 1.0 fusion.2.normed_ref
  12.4 0.8 copy-done.3
  13.3 0.0 copy-start.1
  13.3 2.1 convolution_convert_fusion.value_ref
  15.4 2.0 convolution_convert_fusion.1.key_ref
  17.5 0.0 copy-done.1
  17.5 1.0 slice_bitcast_fusion.w_ref
  18.5 41.4 %shard_map.73 = (bf16[4096,256]{1,0:T(8,128)(2,1)}, bf16[4096,256]{1,0:T(8,128)(2,1)}, s32[4,8,128]{2,1,0:T(8,128)}, bf16[1024,256]{1,0:T(8,128)(2,1)}) custom-call(bf16[1024,256]{1,0:T(8,128)(2,1)} %convolution_convert_fusion.1.key_ref, bf16[1024,256]{1,0:T(8,128)(2,1)} %convolution_convert_fusion.value_ref, s32[8,128]{1,0:T(8,128)} %bitcast.15, ...), custom_call_target="tpu_custom_call" | custom-call | tf_op jit(solution)/shard_map/pallas_call | solution.py:109
  59.9 0.0 copy-done.7
  59.9 2.5 convert_reduce_fusion
  62.4 0.1 fusion.14
  62.5 0.6 pad_add_fusion.table
  63.1 0.6 add_add_fusion.pos_ref
  63.7 2.3 constant_dynamic-slice_fusion
  66.0 0.0 copy-done.6
  66.0 11.1 %shard_map.74 = (bf16[1024,256]{1,0:T(8,128)(2,1)}, f32[2,2,512]{2,1,0:T(2,128)}) custom-call(s32[2,4]{1,0:T(2,128)} %pad_add_fusion.table, bf16[1024,256]{1,0:T(8,128)(2,1)} %get-tuple-element.16.query_ref, bf16[4096,256]{1,0:T(8,128)(2,1)} %get-tuple-element.17.key_ref, bf16[4096,256]{1,0:T(8,128)(2,1)} %get-tuple-element.18.value_ref, ...), custom_call_target="tpu_custom_call" | custom-call | flops 4294967296 | tf_op jit(solution)/shard_map/pallas_call | solution.py:556
  77.0 13.0 %all-gather.2.cloned.1.call-done.w_any = bf16[2048,2048]{1,0:T(8,128)(2,1)} async-done(((bf16[256,2048]{1,0:T(8,128)(2,1)}), bf16[2048,2048]{1,0:T(8,128)(2,1)}) %all-gather.2.cloned.1.call-update) | async-done | bytes 8388624 | tf_op jit(solution)/shard_map/all_gather | solution.py:534
  90.1 36.1 %shard_map.75 = (bf16[1024,256]{1,0:T(8,128)(2,1)}, f32[128,2048]{1,0:T(8,128)}) custom-call(bf16[1024,256]{1,0:T(8,128)(2,1)} %get-tuple-element.19.part_ref.out_ref, bf16[2048,2048]{1,0:T(8,128)(2,1)} %all-gather.2.cloned.1.call-done.w_any, bf16[128,2048]{1,0:T(8,128)(2,1)} %get-tuple-element.34.state_ref, bf16[128,2048]{1,0:T(8,128)(2,1)} %get-tuple-element.33.probe_ref), custom_call_target="tpu_custom_call" | custom-call | tf_op jit(solution)/shard_map/pallas_call | solution.py:358
  126.2 16.2 %shard_map.76 = (bf16[1024,256]{1,0:T(8,128)(2,1)}, bf16[4096,512]{1,0:T(8,128)(2,1)}) custom-call(s32[2,4]{1,0:T(2,128)} %pad_add_fusion.table, bf16[1024,256]{1,0:T(8,128)(2,1)} %get-tuple-element.16.query_ref, bf16[4096,256]{1,0:T(8,128)(2,1)} %get-tuple-element.17.key_ref, bf16[4096,256]{1,0:T(8,128)(2,1)} %get-tuple-element.18.value_ref, ...), custom_call_target="tpu_custom_call" | custom-call | flops 10737418240 | tf_op jit(solution)/shard_map/pallas_call | solution.py:581
  142.4 100.5 %shard_map.77 = f32[128,2048]{1,0:T(8,128)} custom-call(bf16[4096,512]{1,0:T(8,128)(2,1)} %get-tuple-element.23.pair_any, bf16[1024,256]{1,0:T(8,128)(2,1)} %get-tuple-element.24.query_ref, bf16[3,2048,256]{2,1,0:T(8,128)(2,1)} %w_ref.1), custom_call_target="tpu_custom_call" | custom-call | tf_op jit(solution)/shard_map/pallas_call | solution.py:498
  243.0 0.0 copy-done.2
  243.0 1.5 fusion.3
  244.5 0.0 copy-done.4
  244.5 0.0 copy-done.5
  244.5 2.8 %fusion.8 = f32[128,2048]{1,0:T(8,128)} fusion(bf16[128,2048]{1,0:T(8,128)(2,1)S(1)} %copy-done.2, bf16[128,2048]{1,0:T(8,128)(2,1)S(1)} %copy-done.5, f32[128,2048]{1,0:T(8,128)S(1)} %copy-done.4, f32[128,2048]{1,0:T(8,128)} %shard_map.77, f32[128]{0:T(128)S(1)} %broadcast_multiply_fusion, f32[128]{0:T(128)S(1)} %get-tuple-element.32, ...), kind=kLoop, calls=%fused_computation.17 | loop fusion | flops 3145728 | bytes 4204032 | tf_op jit(solution)/shard_map/add | solution.py:612
  (10 shorter events, 0.0 us)
Async XLA Ops:
  6.5 83.5 %all-gather.2.cloned.1.call-start = ((), (), s32[]{:S(2)}) async-start(), calls=%async_computation | async-start | bytes 9437184 | tf_op jit(solution)/shard_map/all_gather | solution.py:534
  7.3 4.1 %copy-start = (bf16[1024,2048]{1,0:T(8,128)(2,1)S(1)}, bf16[1024,2048]{1,0:T(8,128)(2,1)}, u32[]{:S(2)}) copy-start(bf16[1024,2048]{1,0:T(8,128)(2,1)} %param.7) | copy-start | bytes 12582916
  11.4 1.9 copy-start.3
  13.3 4.2 %copy-start.1 = (bf16[1024,2048]{1,0:T(8,128)(2,1)}, bf16[1024,2048]{1,0:T(8,128)(2,1)S(1)}, u32[]{:S(2)}) copy-start(bf16[1024,2048]{1,0:T(8,128)(2,1)S(1)} %fusion.2.normed_ref) | copy-start | bytes 12582916
  17.5 42.4 %copy-start.7 = (s32[1024]{0:T(1024)S(1)}, s32[1024]{0:T(1024)}, u32[]{:S(2)}) copy-start(s32[1024]{0:T(1024)} %param.13) | copy-start | bytes 12292
  62.4 3.6 %copy-start.6 = (s32[1024]{0:T(1024)}, s32[1024]{0:T(1024)S(1)}, u32[]{:S(2)}) copy-start(s32[1024]{0:T(1024)S(1)} %convert_reduce_fusion) | copy-start | bytes 12292
  142.4 100.5 %copy-start.2 = (bf16[128,2048]{1,0:T(8,128)(2,1)S(1)}, bf16[128,2048]{1,0:T(8,128)(2,1)}, u32[]{:S(2)}) copy-start(bf16[128,2048]{1,0:T(8,128)(2,1)} %get-tuple-element.34.state_ref) | copy-start | bytes 1572868
  142.4 102.1 %copy-start.4 = (f32[128,2048]{1,0:T(8,128)S(1)}, f32[128,2048]{1,0:T(8,128)}, u32[]{:S(2)}) copy-start(f32[128,2048]{1,0:T(8,128)} %get-tuple-element.20) | copy-start | bytes 3145732
  142.4 102.1 %copy-start.5 = (bf16[128,2048]{1,0:T(8,128)(2,1)S(1)}, bf16[128,2048]{1,0:T(8,128)(2,1)}, u32[]{:S(2)}) copy-start(bf16[128,2048]{1,0:T(8,128)(2,1)} %param.12) | copy-start | bytes 1572868
Sparse Core Ops, SparseCore 0:
  8.9 81.1 all-gather.1
where the time goes:
time: 252 us; the launch traced here: 254 us
  Pallas kernels  205 us (81%)
  waiting for transfers between devices  13.7 us (5%)
  between operations  13.5 us (5%)
  other arithmetic  13.3 us (5%)
  local copies, waits for them, and re-layouts  4.2 us (2%)
  matrix products  4.17 us (2%)
    pallas_call x1, Pallas kernels, tail(): pl.pallas_call(functools.partial(tail_kernel, ctx_count, number), out_sha...  101 us
    pallas_call x1, Pallas kernels, gather_keys(): pl.pallas_call(functools.partial(gather_kernel, number), out_shape=(full,...  41.4 us
    pallas_call x1, Pallas kernels, middle(): pl.pallas_call(functools.partial(middle_kernel, number), out_shape=(jax.S...  36.1 us
    pallas_call x1, Pallas kernels, body(): pl.pallas_call(functools.partial(backward_kernel, local_heads, gq, gk), o...  16.2 us
    all_gather x1, waiting for transfers between devices, body(): w_full = lax.all_gather(w_out, 'head', axis=0, tiled=True)  13 us
    pallas_call x1, Pallas kernels, body(): pl.pallas_call(functools.partial(forward_kernel, local_heads, fq, fk), ou...  11.1 us
  transfers between devices with their start and end apart: 1, of which 1 were waited for; matrix products, arithmetic and copies ran while one was open for 6% of the time, Pallas kernels for 21%

commit v1 on v0

--- a/solution.py
+++ b/solution.py
@@ -10,6 +10,7 @@
 HEAD_DIM = 128
 EPSILON = 1e-05
 STEP_SIZE = 0.25
+NOISE_SCALE = (2.0 * STEP_SIZE) ** 0.5
 NEGATIVE = -1e30
 LOG2E = 1.4426950408889634
 MESH = pl.DeviceIdType.MESH
@@ -612,6 +613,853 @@
     return state_own - STEP_SIZE * gradient + jnp.sqrt(2.0 * STEP_SIZE) * noise.astype(jnp.float32)
 
 
+def remote(source, target, send_sem, recv_sem, ctx, head):
+    return pltpu.make_async_remote_copy(
+        src_ref=source,
+        dst_ref=target,
+        send_sem=send_sem,
+        recv_sem=recv_sem,
+        device_id={"ctx": ctx, "head": head},
+        device_id_type=MESH,
+    )
+
+
+def place():
+    ctx, me = lax.axis_index("ctx"), lax.axis_index("head")
+    return ctx, me, me // 2, lax.rem(me, 2)
+
+
+def meet(peers):
+    barrier = pltpu.get_barrier_semaphore()
+    for ctx, head in peers:
+        pl.semaphore_signal(
+            barrier, inc=1, device_id={"ctx": ctx, "head": head}, device_id_type=MESH
+        )
+    pl.semaphore_wait(barrier, len(peers))
+
+
+def far_first(groups, group, step):
+    result = 0
+    for index in range(groups):
+        order = sorted(range(groups), key=lambda other: (-abs(other - index), -other))
+        result = jnp.where(group == index, order[step], result)
+    return result
+
+
+def project_kernel(
+    ctx_count, head_count, state_any, w_any, gain_ref, seg_ref, query_out, kv_out, segs_out,
+    state_v, w_v, query_buf, kv_buf, state_sem, w_sem, q_send, q_recv, kv_send, kv_recv, pass_send,
+    seg_send, seg_recv, own_q, own_kv, own_seg,
+):
+    ctx, me, group, core = place()
+    rows, model = state_any.shape
+    own, groups = rows // head_count, head_count // 2
+    slots = w_any.shape[2] // HEAD_DIM
+    chunk = 2 * own
+    partner = group * 2 + 1 - core
+
+    def at(piece):
+        return pl.ds(pl.multiple_of(piece * chunk, chunk), chunk)
+
+    def load_state(piece):
+        return pltpu.make_async_copy(
+            state_any.at[at(piece)], state_v.at[at(piece)], state_sem.at[piece]
+        )
+
+    load_state(0).start()
+    w_loads = [pltpu.make_async_copy(w_any.at[t], w_v.at[t], w_sem.at[t]) for t in range(3)]
+    for copy in w_loads:
+        copy.start()
+    for piece in range(1, groups):
+        load_state(piece).start()
+    peers = [(lax.rem(ctx + step, ctx_count), me) for step in range(1, ctx_count)]
+    peers += [(lax.rem(ctx + step, ctx_count), partner) for step in range(ctx_count)]
+    meet(peers)
+    segs = []
+    for step in range(1, ctx_count):
+        copy = remote(
+            seg_ref, segs_out.at[ctx], seg_send.at[step], seg_recv.at[step],
+            lax.rem(ctx + step, ctx_count), me,
+        )
+        copy.start()
+        segs.append(copy)
+    copy = pltpu.make_async_copy(seg_ref, segs_out.at[ctx], own_seg)
+    copy.start()
+    segs.append(copy)
+    for copy in w_loads:
+        copy.wait()
+    gain = gain_ref[...].astype(jnp.float32)
+
+    def away(slot, kind, piece, dest):
+        head = group * 2 + kind
+        return (
+            remote(
+                query_buf.at[slot, piece, kind], query_out.at[ctx, piece],
+                q_send.at[slot, kind, piece], q_recv.at[ctx, piece], dest, head,
+            ),
+            remote(
+                kv_buf.at[slot, kind, piece], kv_out.at[kind, ctx, piece],
+                kv_send.at[slot, kind, piece], kv_recv.at[kind, ctx, piece], dest, head,
+            ),
+        )
+
+    def local(slot, piece):
+        result = [
+            pltpu.make_async_copy(
+                query_buf.at[slot, piece, core], query_out.at[ctx, piece], own_q.at[piece]
+            )
+        ]
+        for kind in range(2):
+            result.append(
+                pltpu.make_async_copy(
+                    kv_buf.at[slot, kind, piece], kv_out.at[kind, ctx, piece],
+                    own_kv.at[kind, piece],
+                )
+            )
+        return result
+
+    def beside(slot, piece):
+        result = [
+            remote(
+                query_buf.at[slot, piece, 1 - core], query_out.at[ctx, piece],
+                q_send.at[slot, 1 - core, piece], q_recv.at[ctx, piece], ctx, partner,
+            )
+        ]
+        for kind in range(2):
+            result.append(
+                remote(
+                    kv_buf.at[slot, kind, piece], kv_out.at[kind, ctx, piece],
+                    kv_send.at[slot, kind, piece], kv_recv.at[kind, ctx, piece], ctx, partner,
+                )
+            )
+        return result
+
+    def project(piece, _):
+        load_state(piece).wait()
+        block = state_v[at(piece), :].astype(jnp.float32)
+        normed = (block * row_scale(block) * gain).astype(jnp.bfloat16)
+        for t in range(3):
+            result = jnp.dot(normed, w_v[t], preferred_element_type=jnp.float32).astype(
+                jnp.bfloat16
+            )
+            for slot in range(slots):
+                part = result[:, slot * HEAD_DIM : (slot + 1) * HEAD_DIM]
+                if t == 0:
+                    query_buf[slot, piece, 0] = part[:own]
+                    query_buf[slot, piece, 1] = part[own:]
+                else:
+                    kv_buf[slot, t - 1, piece] = part
+        for slot in range(slots):
+            dest = core * slots + slot
+
+            @pl.when(dest != ctx)
+            def _():
+                for kind in range(2):
+                    for copy in away(slot, kind, piece, dest):
+                        copy.start()
+
+            @pl.when(dest == ctx)
+            def _():
+                for copy in local(slot, piece) + beside(slot, piece):
+                    copy.start()
+
+        return 0
+
+    lax.fori_loop(0, groups, project, 0)
+
+    def hand_over(piece, step):
+        source = lax.rem(ctx + step, ctx_count)
+        return remote(
+            kv_out.at[core, source, piece], kv_out.at[core, source, piece],
+            pass_send.at[step, piece], kv_recv.at[core, source, piece], ctx, partner,
+        )
+
+    def forward(piece, _):
+        for step in range(1, ctx_count):
+            copy = hand_over(piece, step)
+            copy.wait_recv()
+            copy.start()
+        return 0
+
+    lax.fori_loop(0, groups, forward, 0)
+
+    def got_query(source, piece):
+        remote(
+            query_out.at[source, piece], query_out.at[source, piece], q_send.at[0, 0, piece],
+            q_recv.at[source, piece], ctx, partner,
+        ).wait_recv()
+
+    def got_kv(kind, source, piece):
+        remote(
+            kv_out.at[kind, source, piece], kv_out.at[kind, source, piece],
+            kv_send.at[0, 0, piece], kv_recv.at[kind, source, piece], ctx, partner,
+        ).wait_recv()
+
+    mine = ctx // slots == core
+
+    def finish(piece, _):
+        for step in range(1, ctx_count):
+            source = lax.rem(ctx + step, ctx_count)
+            got_query(source, piece)
+            got_kv(1 - core, source, piece)
+            hand_over(piece, step).wait_send()
+        for slot in range(slots):
+            dest = core * slots + slot
+
+            @pl.when(dest != ctx)
+            def _():
+                for kind in range(2):
+                    for copy in away(slot, kind, piece, dest):
+                        copy.wait_send()
+
+            @pl.when(dest == ctx)
+            def _():
+                for copy in local(slot, piece):
+                    copy.wait()
+                for copy in beside(slot, piece):
+                    copy.wait_send()
+
+        @pl.when(jnp.logical_not(mine))
+        def _():
+            got_query(ctx, piece)
+            for kind in range(2):
+                got_kv(kind, ctx, piece)
+
+        return 0
+
+    lax.fori_loop(0, groups, finish, 0)
+    for copy in segs:
+        copy.wait()
+
+
+def project_heads(ctx_count, head_count, state, w_qkv, gain, segment_ids):
+    rows, model = state.shape
+    width = w_qkv.shape[2]
+    own, groups, slots = rows // head_count, head_count // 2, width // HEAD_DIM
+    seg = segment_ids.reshape(-1, 128)
+    half, dma = jnp.bfloat16, pltpu.SemaphoreType.DMA
+    return pl.pallas_call(
+        functools.partial(project_kernel, ctx_count, head_count),
+        out_shape=(
+            jax.ShapeDtypeStruct((ctx_count, groups, own, HEAD_DIM), half),
+            jax.ShapeDtypeStruct((2, ctx_count, groups, 2 * own, HEAD_DIM), half),
+            jax.ShapeDtypeStruct((ctx_count,) + seg.shape, seg.dtype),
+        ),
+        in_specs=[ANY, ANY, VMEM, VMEM],
+        out_specs=(ANY, ANY, ANY),
+        scratch_shapes=[
+            pltpu.VMEM((rows, model), half),
+            pltpu.VMEM(w_qkv.shape, half),
+            pltpu.VMEM((slots, groups, 2, own, HEAD_DIM), half),
+            pltpu.VMEM((slots, 2, groups, 2 * own, HEAD_DIM), half),
+            dma((groups,)),
+            dma((3,)),
+            dma((slots, 2, groups)),
+            dma((ctx_count, groups)),
+            dma((slots, 2, groups)),
+            dma((2, ctx_count, groups)),
+            dma((ctx_count, groups)),
+            dma((ctx_count,)),
+            dma((ctx_count,)),
+            dma((groups,)),
+            dma((2, groups)),
+            dma,
+        ],
+        compiler_params=pltpu.CompilerParams(
+            collective_id=0, has_side_effects=True, vmem_limit_bytes=60 * 2**20
+        ),
+    )(state, w_qkv, gain, seg)
+
+
+def segment_bounds(segs_ref):
+    segs = segs_ref[...]
+
+    def below(value):
+        return jnp.sum(jnp.where(segs < value, 1.0, 0.0)).astype(jnp.int32)
+
+    return below(1), below(2)
+
+
+def tile_plan(bounds, rows, own, parts, sub, bk, tile, core):
+    first_bound, second_bound = bounds
+
+    def start_of(pos):
+        return jnp.where(pos >= second_bound, second_bound, jnp.where(pos >= first_bound, first_bound, 0))
+
+    blocks = sub // own
+    base = tile * rows + core * own
+    places = []
+    for part in range(parts):
+        lane = lax.broadcasted_iota(jnp.int32, (1, sub), 1)
+        pos = base + (lane // own + part * blocks) * (2 * own) + lane % own
+        places.append((start_of(pos), pos))
+    first, last = base, base + (parts * blocks - 1) * 2 * own + own - 1
+    low = start_of(first) // bk
+    inner_low = (start_of(last) + bk - 1) // bk
+    inner_high = jnp.maximum(inner_low, (first + 1) // bk)
+    high = last // bk + 1
+    return places, low, inner_low, inner_high, high
+
+
+def head_forward_kernel(
+    rows, own, parts, sub, bk, segs_ref, query_ref, kv_ref, out_ref, log_ref
+):
+    factor = HEAD_DIM ** (-0.5) * LOG2E
+    core = lax.rem(lax.axis_index("head"), 2)
+    bounds = segment_bounds(segs_ref)
+    tiles = query_ref.shape[0] // (parts * sub)
+
+    def one_tile(tile, _):
+        places, low, inner_low, inner_high, high = tile_plan(
+            bounds, rows, own, parts, sub, bk, tile, core
+        )
+
+        def at(part):
+            return pl.ds(pl.multiple_of((tile * parts + part) * sub, sub), sub)
+
+        def step(masked, piece, carry):
+            keys_at = pl.ds(pl.multiple_of(piece * bk, bk), bk)
+            if masked:
+                key_pos = piece * bk + lax.broadcasted_iota(jnp.int32, (bk, sub), 0)
+            result = []
+            for part in range(parts):
+                top, total, acc = carry[part]
+                scores = dot32(kv_ref[0, keys_at, :], query_ref[at(part), :], NT)
+                if masked:
+                    start, pos = places[part]
+                    scores = jnp.where((key_pos >= start) & (key_pos <= pos), scores, NEGATIVE)
+                new_top = jnp.maximum(top, jnp.max(scores, axis=0, keepdims=True) * factor)
+                weights = jnp.exp2(scores * factor - new_top)
+                scale = jnp.exp2(top - new_top)
+                total = total * scale + jnp.sum(weights, axis=0, keepdims=True)
+                acc = acc * scale + dot32(kv_ref[1, keys_at, :], weights.astype(jnp.bfloat16), TN)
+                result.append((new_top, total, acc))
+            return tuple(result)
+
+        carry = tuple(
+            (
+                jnp.full((1, sub), NEGATIVE, jnp.float32),
+                jnp.zeros((1, sub), jnp.float32),
+                jnp.zeros((HEAD_DIM, sub), jnp.float32),
+            )
+            for _ in range(parts)
+        )
+        carry = lax.fori_loop(low, inner_low, functools.partial(step, True), carry)
+        carry = lax.fori_loop(inner_low, inner_high, functools.partial(step, False), carry)
+        carry = lax.fori_loop(inner_high, high, functools.partial(step, True), carry)
+        for part in range(parts):
+            top, total, acc = carry[part]
+            out_ref[at(part), :] = (acc / total).T.astype(jnp.bfloat16)
+            log_ref[tile, pl.ds(part, 1), :] = top + jnp.log2(total)
+        return 0
+
+    lax.fori_loop(0, tiles, one_tile, 0)
+
+
+def head_backward_kernel(
+    rows, own, parts, sub, bk, segs_ref, query_ref, kv_ref, grad_ref, out_ref, log_ref, query_out,
+    pair_out, pair_acc,
+):
+    score_scale = HEAD_DIM ** (-0.5)
+    factor = score_scale * LOG2E
+    core = lax.rem(lax.axis_index("head"), 2)
+    bounds = segment_bounds(segs_ref)
+    tiles = query_ref.shape[0] // (parts * sub)
+    pair_rows = pair_acc.shape[0]
+
+    def clear(piece, _):
+        at = pl.ds(pl.multiple_of(piece * bk, bk), bk)
+        pair_acc[at, :] = jnp.zeros((bk, 2 * HEAD_DIM), jnp.float32)
+        return 0
+
+    lax.fori_loop(0, pair_rows // bk, clear, 0)
+
+    def one_tile(tile, _):
+        places, low, inner_low, inner_high, high = tile_plan(
+            bounds, rows, own, parts, sub, bk, tile, core
+        )
+
+        def at(part):
+            return pl.ds(pl.multiple_of((tile * parts + part) * sub, sub), sub)
+
+        deltas, logs = [], []
+        for part in range(parts):
+            product = grad_ref[at(part), :].astype(jnp.float32) * out_ref[at(part), :].astype(
+                jnp.float32
+            )
+            deltas.append(jnp.sum(product.T, axis=0, keepdims=True))
+            logs.append(log_ref[tile, pl.ds(part, 1), :])
+
+        def step(masked, piece, carry):
+            keys_at = pl.ds(pl.multiple_of(piece * bk, bk), bk)
+            if masked:
+                key_pos = piece * bk + lax.broadcasted_iota(jnp.int32, (bk, sub), 0)
+            result = []
+            key_block, value_block = kv_ref[0, keys_at, :], kv_ref[1, keys_at, :]
+            for part in range(parts):
+                query_block, grad_block = query_ref[at(part), :], grad_ref[at(part), :]
+                scores = dot32(key_block, query_block, NT)
+                probabilities = jnp.exp2(scores * factor - logs[part])
+                if masked:
+                    start, pos = places[part]
+                    probabilities = jnp.where(
+                        (key_pos >= start) & (key_pos <= pos), probabilities, 0.0
+                    )
+                dprobs = dot32(value_block, grad_block, NT)
+                dscores = (probabilities * (dprobs - deltas[part])).astype(jnp.bfloat16)
+                pair_acc[keys_at, HEAD_DIM:] += jnp.dot(
+                    probabilities.astype(jnp.bfloat16),
+                    grad_block,
+                    preferred_element_type=jnp.float32,
+                )
+                pair_acc[keys_at, :HEAD_DIM] += jnp.dot(
+                    dscores, query_block, preferred_element_type=jnp.float32
+                )
+                result.append(carry[part] + dot32(key_block, dscores, TN))
+            return tuple(result)
+
+        carry = tuple(jnp.zeros((HEAD_DIM, sub), jnp.float32) for _ in range(parts))
+        carry = lax.fori_loop(low, inner_low, functools.partial(step, True), carry)
+        carry = lax.fori_loop(inner_low, inner_high, functools.partial(step, False), carry)
+        carry = lax.fori_loop(inner_high, high, functools.partial(step, True), carry)
+        for part in range(parts):
+            query_out[at(part), :] = (carry[part].T * score_scale).astype(jnp.bfloat16)
+        return 0
+
+    lax.fori_loop(0, tiles, one_tile, 0)
+
+    def flush(piece, _):
+        at = pl.ds(pl.multiple_of(piece * bk, bk), bk)
+        pair_out[at, :HEAD_DIM] = (pair_acc[at, :HEAD_DIM] * score_scale).astype(jnp.bfloat16)
+        pair_out[at, HEAD_DIM:] = pair_acc[at, HEAD_DIM:].astype(jnp.bfloat16)
+        return 0
+
+    lax.fori_loop(0, pair_rows // bk, flush, 0)
+
+
+def readout_kernel(
+    ctx_count, head_count, part_ref, w_any, state_any, probe_any, grad_out, readout_out, w_ref,
+    joined, half, sending, state_own, probe_own, out_send, out_recv, back_send, back_recv, own_sem,
+    w_sem, row_sem,
+):
+    ctx, me, group, core = place()
+    groups = head_count // 2
+    own, model = readout_out.shape
+    my_rows = pl.ds(pl.multiple_of(me * own, own), own)
+    row_loads = [
+        pltpu.make_async_copy(state_any.at[my_rows], state_own, row_sem.at[0]),
+        pltpu.make_async_copy(probe_any.at[my_rows], probe_own, row_sem.at[1]),
+    ]
+    for copy in row_loads:
+        copy.start()
+    quarter = w_any.shape[2]
+
+    def load_w(index):
+        piece, head = index // head_count, lax.rem(index, head_count)
+        first = pl.multiple_of((head * ctx_count + piece) * quarter, quarter)
+        return pltpu.make_async_copy(
+            w_any.at[piece, head], w_ref.at[pl.ds(first, quarter)], w_sem.at[index]
+        )
+
+    def start_w(index, _):
+        load_w(index).start()
+        return 0
+
+    def wait_w(index, _):
+        load_w(index).wait()
+        return 0
+
+    lax.fori_loop(0, ctx_count * head_count, start_w, 0)
+    peers = []
+    for far in range(groups):
+        for step in range(ctx_count):
+            if far or step:
+                peers.append(
+                    (lax.rem(ctx + step, ctx_count), lax.rem(group + far, groups) * 2 + core)
+                )
+    meet(peers)
+
+    def cols_of(group_at, ctx_at):
+        head = group_at * ctx_count + ctx_at
+        return pl.ds(pl.multiple_of(head * HEAD_DIM, HEAD_DIM), HEAD_DIM)
+
+    copies = []
+    for order in range(groups):
+        other = far_first(groups, group, order)
+        for step in range(ctx_count):
+            peer = lax.rem(ctx + step, ctx_count)
+            if order == groups - 1 and step == 0:
+                continue
+            copy = remote(
+                part_ref.at[peer, other], joined.at[:, cols_of(group, ctx)],
+                out_send.at[order, step], out_recv.at[group, ctx], peer, other * 2 + core,
+            )
+            copy.start()
+            copies.append(copy)
+    joined[:, cols_of(group, ctx)] = part_ref[ctx, group]
+    for copy in row_loads:
+        copy.wait()
+    lax.fori_loop(0, ctx_count * head_count, wait_w, 0)
+    sources = []
+    for far in range(groups):
+        for step in range(ctx_count):
+            if far or step:
+                sources.append((lax.rem(group + far, groups), lax.rem(ctx + step, ctx_count)))
+    for other, peer in sources:
+        remote(
+            part_ref.at[peer, other], joined.at[:, cols_of(other, peer)], out_send.at[0, 0],
+            out_recv.at[other, peer], peer, other * 2 + core,
+        ).wait_recv()
+    for copy in copies:
+        copy.wait_send()
+    tile = min(256, model)
+
+    def project(piece, carry):
+        squares, products = carry
+        cols = pl.ds(pl.multiple_of(piece * tile, tile), tile)
+        layer = state_own[:, cols].astype(jnp.float32) + jnp.dot(
+            joined[...], w_ref[:, cols], preferred_element_type=jnp.float32
+        )
+        readout_out[:, cols] = layer
+        squares = squares + jnp.sum(layer * layer, axis=1, keepdims=True)
+        products = products + jnp.sum(
+            layer * probe_own[:, cols].astype(jnp.float32), axis=1, keepdims=True
+        )
+        return squares, products
+
+    zero = jnp.zeros((own, 1), jnp.float32)
+    squares, products = lax.fori_loop(0, model // tile, project, (zero, zero))
+    scale = lax.rsqrt(squares / model + EPSILON)
+    bend = scale**3 * (products / model)
+
+    def finish(piece, _):
+        cols = pl.ds(pl.multiple_of(piece * tile, tile), tile)
+        readout = scale * probe_own[:, cols].astype(jnp.float32) - readout_out[:, cols] * bend
+        readout_out[:, cols] = readout
+        half[:, cols] = readout.astype(jnp.bfloat16)
+        return 0
+
+    lax.fori_loop(0, model // tile, finish, 0)
+    wide = ctx_count * HEAD_DIM
+    copies = []
+    for order in range(groups):
+        other = far_first(groups, group, order)
+        result = dot32(
+            half[...], w_ref[pl.ds(pl.multiple_of(other * wide, wide), wide), :], NT
+        ).astype(jnp.bfloat16)
+        for index in range(ctx_count):
+            sending[order, index] = result[:, index * HEAD_DIM : (index + 1) * HEAD_DIM]
+        for step in range(ctx_count):
+            peer = lax.rem(ctx + step, ctx_count)
+            if order == groups - 1 and step == 0:
+                continue
+            copy = remote(
+                sending.at[order, peer], grad_out.at[ctx, group], back_send.at[order, step],
+                back_recv.at[ctx, group], peer, other * 2 + core,
+            )
+            copy.start()
+            copies.append(copy)
+    copy = pltpu.make_async_copy(sending.at[groups - 1, ctx], grad_out.at[ctx, group], own_sem)
+    copy.start()
+    for other, peer in sources:
+        remote(
+            sending.at[0, 0], grad_out.at[peer, other], back_send.at[0, 0],
+            back_recv.at[peer, other], peer, other * 2 + core,
+        ).wait_recv()
+    for remote_copy in copies:
+        remote_copy.wait_send()
+    copy.wait()
+
+
+def readout_step(ctx_count, head_count, part, w_full, state, probe):
+    rows, model = state.shape
+    own, groups = rows // head_count, head_count // 2
+    half, full, dma = jnp.bfloat16, jnp.float32, pltpu.SemaphoreType.DMA
+    return pl.pallas_call(
+        functools.partial(readout_kernel, ctx_count, head_count),
+        out_shape=(
+            jax.ShapeDtypeStruct(part.shape, half),
+            jax.ShapeDtypeStruct((own, model), full),
+        ),
+        in_specs=[VMEM, ANY, ANY, ANY],
+        out_specs=(ANY, VMEM),
+        scratch_shapes=[
+            pltpu.VMEM((model, model), half),
+            pltpu.VMEM((own, model), half),
+            pltpu.VMEM((own, model), half),
+            pltpu.VMEM((groups, ctx_count, own, HEAD_DIM), half),
+            pltpu.VMEM((own, model), half),
+            pltpu.VMEM((own, model), half),
+            dma((groups, ctx_count)),
+            dma((groups, ctx_count)),
+            dma((groups, ctx_count)),
+            dma((ctx_count, groups)),
+            dma,
+            dma((ctx_count * head_count,)),
+            dma((2,)),
+        ],
+        compiler_params=pltpu.CompilerParams(
+            collective_id=1, has_side_effects=True, vmem_limit_bytes=60 * 2**20
+        ),
+    )(part, w_full, state, probe)
+
+
+def finish_kernel(
+    ctx_count, head_count, query_ref, pair_ref, w_any, state_any, noise_ref, readout_ref, gain_ref,
+    new_out, w_both, beside, away, terms_in, partial, sending, total, state_own, b_send, b_recv,
+    w_send, w_recv, a_send, a_recv, z_send, z_recv, own_sem,
+):
+    ctx, me, group, core = place()
+    groups = head_count // 2
+    own, model = new_out.shape
+    slots = ctx_count // 2
+    partner = group * 2 + 1 - core
+    my_rows = pl.ds(pl.multiple_of(me * own, own), own)
+    loads = [
+        pltpu.make_async_copy(w_any, w_both.at[core], own_sem.at[0]),
+        pltpu.make_async_copy(state_any.at[my_rows], state_own, own_sem.at[1]),
+    ]
+    for copy in loads:
+        copy.start()
+    peers = [(ctx, partner)]
+    peers += [(lax.rem(ctx + step, ctx_count), me) for step in range(1, ctx_count)]
+    peers += [(ctx, lax.rem(group + far, groups) * 2 + core) for far in range(1, groups)]
+    meet(peers)
+    dests = [far_first(groups, group, order) for order in range(groups)]
+    copies = []
+    for order, dest in enumerate(dests):
+        copy = remote(
+            pair_ref.at[:, dest, 1 - core], beside.at[order], b_send.at[order], b_recv.at[order],
+            ctx, partner,
+        )
+        copy.start()
+        copies.append(copy)
+    w_copy = remote(w_any, w_both.at[core], w_send, w_recv, ctx, partner)
+    w_copy.start()
+
+    def stripe(source):
+        slot = lax.rem(source, slots)
+        return pl.ds(pl.multiple_of(slot * HEAD_DIM, HEAD_DIM), HEAD_DIM)
+
+    def exchange(order, dest, step):
+        peer = lax.rem(ctx + step, ctx_count)
+        return remote(
+            away.at[order, step], terms_in.at[dest, ctx // slots, :, :, stripe(ctx)],
+            a_send.at[order, step], a_recv.at[dest, ctx], peer, me,
+        )
+
+    def arrived(dest, step):
+        source = lax.rem(ctx + step, ctx_count)
+        remote(
+            away.at[0, 0], terms_in.at[dest, source // slots, :, :, stripe(source)],
+            a_send.at[0, 0], a_recv.at[dest, source], source, me,
+        ).wait_recv()
+
+    for order, dest in enumerate(dests):
+        copies[order].wait_recv()
+        for step in range(1, ctx_count):
+            peer = lax.rem(ctx + step, ctx_count)
+            pair = pair_ref[peer, dest, core].astype(jnp.float32) + beside[order, peer].astype(
+                jnp.float32
+            )
+            pair = pair.astype(jnp.bfloat16)
+            away[order, step, 0] = query_ref[peer, dest]
+            away[order, step, 1] = pair[:, :HEAD_DIM]
+            away[order, step, 2] = pair[:, HEAD_DIM:]
+            exchange(order, dest, step).start()
+        pair = pair_ref[ctx, dest, core].astype(jnp.float32) + beside[order, ctx].astype(
+            jnp.float32
+        )
+        pair = pair.astype(jnp.bfloat16)
+        at = stripe(ctx)
+        terms_in[dest, ctx // slots, 0, :, at] = query_ref[ctx, dest]
+        terms_in[dest, ctx // slots, 1, :, at] = pair[:, :HEAD_DIM]
+        terms_in[dest, ctx // slots, 2, :, at] = pair[:, HEAD_DIM:]
+    for copy in loads:
+        copy.wait()
+    w_copy.wait()
+    pieces = partial.shape[2]
+    tile = model // pieces
+
+    def chain(order, dest, piece):
+        up = dest > group
+        line = jnp.where(up, 0, 1)
+        peer = jnp.where(up, group + 1, group - 1)
+        return remote(
+            sending.at[order, piece], partial.at[line, dest, piece], z_send.at[order, piece],
+            z_recv.at[line, dest, piece], ctx, peer * 2 + core,
+        )
+
+    def came(line, dest, piece):
+        remote(
+            sending.at[0, piece], partial.at[line, dest, piece], z_send.at[0, piece],
+            z_recv.at[line, dest, piece], ctx, partner,
+        ).wait_recv()
+
+    def term(dest, piece):
+        cols = pl.ds(pl.multiple_of(piece * tile, tile), tile)
+        result = None
+        for half in range(2):
+            for kind in range(3):
+                part = dot32(terms_in[dest, half, kind], w_both[half, kind, cols, :], NT)
+                result = part if result is None else result + part
+        return result
+
+    for order, dest in enumerate(dests[:-1]):
+        for step in range(1, ctx_count):
+            arrived(dest, step)
+        line = jnp.where(dest > group, 0, 1)
+        inner = (group > 0) & (group < groups - 1)
+
+        def one_piece(piece, _):
+            total[...] = term(dest, piece)
+
+            @pl.when(inner)
+            def _():
+                came(line, dest, piece)
+                total[...] += partial[line, dest, piece].astype(jnp.float32)
+
+            sending[order, piece] = total[...].astype(jnp.bfloat16)
+            chain(order, dest, piece).start()
+            return 0
+
+        lax.fori_loop(0, pieces, one_piece, 0)
+
+    for step in range(1, ctx_count):
+        arrived(group, step)
+
+    state = state_own[...].astype(jnp.float32)
+    inverse = row_scale(state)
+
+    def last_piece(piece, slope):
+        cols = pl.ds(pl.multiple_of(piece * tile, tile), tile)
+        total[...] = term(group, piece)
+
+        @pl.when(group > 0)
+        def _():
+            came(0, group, piece)
+            total[...] += partial[0, group, piece].astype(jnp.float32)
+
+        @pl.when(group < groups - 1)
+        def _():
+            came(1, group, piece)
+            total[...] += partial[1, group, piece].astype(jnp.float32)
+
+        gained = total[...] * gain_ref[:, cols].astype(jnp.float32)
+        new_out[:, cols] = gained
+        return slope + jnp.sum(
+            gained * state_own[:, cols].astype(jnp.float32), axis=1, keepdims=True
+        )
+
+    slope = lax.fori_loop(0, pieces, last_piece, jnp.zeros((own, 1), jnp.float32))
+    bend = inverse**3 * (slope / model)
+
+    def update(piece, _):
+        cols = pl.ds(pl.multiple_of(piece * tile, tile), tile)
+        here = state_own[:, cols].astype(jnp.float32)
+        gradient = readout_ref[:, cols] + inverse * new_out[:, cols] - here * bend
+        new_out[:, cols] = (
+            here - STEP_SIZE * gradient + NOISE_SCALE * noise_ref[:, cols].astype(jnp.float32)
+        )
+        return 0
+
+    lax.fori_loop(0, pieces, update, 0)
+    for order, dest in enumerate(dests):
+        copies[order].wait_send()
+        for step in range(1, ctx_count):
+            exchange(order, dest, step).wait_send()
+        if order < groups - 1:
+            for piece in range(pieces):
+                chain(order, dest, piece).wait_send()
+
+
+def finish_step(ctx_count, head_count, query_grad, pair, w_qkv, state, noise, readout, gain):
+    own, model = readout.shape
+    width = w_qkv.shape[2]
+    groups, pieces = head_count // 2, 4
+    half, full, dma = jnp.bfloat16, jnp.float32, pltpu.SemaphoreType.DMA
+    tile = model // pieces
+    return pl.pallas_call(
+        functools.partial(finish_kernel, ctx_count, head_count),
+        out_shape=jax.ShapeDtypeStruct((own, model), full),
+        in_specs=[VMEM, VMEM, ANY, ANY, VMEM, VMEM, VMEM],
+        out_specs=VMEM,
+        scratch_shapes=[
+            pltpu.VMEM((2,) + w_qkv.shape, half),
+            pltpu.VMEM((groups, ctx_count, own, 2 * HEAD_DIM), half),
+            pltpu.VMEM((groups, ctx_count, 3, own, HEAD_DIM), half),
+            pltpu.VMEM((groups, 2, 3, own, width), half),
+            pltpu.VMEM((2, groups, pieces, own, tile), half),
+            pltpu.VMEM((groups, pieces, own, tile), half),
+            pltpu.VMEM((own, tile), full),
+            pltpu.VMEM((own, model), half),
+            dma((groups,)),
+            dma((groups,)),
+            dma,
+            dma,
+            dma((groups, ctx_count)),
+            dma((groups, ctx_count)),
+            dma((groups, pieces)),
+            dma((2, groups, pieces)),
+            dma((2,)),
+        ],
+        compiler_params=pltpu.CompilerParams(
+            collective_id=2, has_side_effects=True, vmem_limit_bytes=60 * 2**20
+        ),
+    )(query_grad, pair, w_qkv, state, noise, readout, gain)
+
+
+def heads_body(state, norm_gain, w_qkv, w_out, probe, noise, segment_ids):
+    rows, model = state.shape
+    head_count, ctx_count = lax.axis_size("head"), lax.axis_size("ctx")
+    own, groups = rows // head_count, head_count // 2
+    quarter = w_out.shape[0] // ctx_count
+    w_part = lax.dynamic_slice_in_dim(w_out, lax.axis_index("ctx") * quarter, quarter, 0)
+    w_full = lax.all_gather(lax.all_gather(w_part, "head", axis=0), "ctx", axis=0)
+    gain = norm_gain.reshape(1, model)
+    queries, kv, segs = project_heads(ctx_count, head_count, state, w_qkv, gain, segment_ids)
+    mine, total = ctx_count * groups * own, ctx_count * rows
+    queries, kv = queries.reshape(mine, HEAD_DIM), kv.reshape(2, total, HEAD_DIM)
+    parts, sub = 2, groups * own // 2
+    tiles, bk = ctx_count, min(rows, 512)
+    params = pltpu.CompilerParams(vmem_limit_bytes=60 * 2**20)
+    outputs, logs = pl.pallas_call(
+        functools.partial(head_forward_kernel, rows, own, parts, sub, bk),
+        out_shape=(
+            jax.ShapeDtypeStruct((mine, HEAD_DIM), jnp.bfloat16),
+            jax.ShapeDtypeStruct((tiles, parts, sub), jnp.float32),
+        ),
+        in_specs=[VMEM] * 3,
+        out_specs=(VMEM, VMEM),
+        compiler_params=params,
+        cost_estimate=pl.CostEstimate(
+            flops=4 * mine * total * HEAD_DIM, bytes_accessed=0, transcendentals=0
+        ),
+    )(segs, queries, kv)
+    shape = (ctx_count, groups, own, HEAD_DIM)
+    grads_out, readout = readout_step(
+        ctx_count, head_count, outputs.reshape(shape), w_full, state, probe
+    )
+    query_grad, pair = pl.pallas_call(
+        functools.partial(head_backward_kernel, rows, own, parts, sub, bk),
+        out_shape=(
+            jax.ShapeDtypeStruct((mine, HEAD_DIM), jnp.bfloat16),
+            jax.ShapeDtypeStruct((total, 2 * HEAD_DIM), jnp.bfloat16),
+        ),
+        in_specs=[VMEM] * 6,
+        out_specs=(VMEM, VMEM),
+        scratch_shapes=[pltpu.VMEM((total, 2 * HEAD_DIM), jnp.float32)],
+        compiler_params=params,
+        cost_estimate=pl.CostEstimate(
+            flops=10 * mine * total * HEAD_DIM, bytes_accessed=0, transcendentals=0
+        ),
+    )(segs, queries, kv, grads_out.reshape(mine, HEAD_DIM), outputs, logs)
+    return finish_step(
+        ctx_count, head_count, query_grad.reshape(shape),
+        pair.reshape(ctx_count, groups, 2, own, 2 * HEAD_DIM), w_qkv, state, noise, readout, gain,
+    )
+
+
 def solution(mesh):
     placed = (
         P("ctx", None),
@@ -622,6 +1470,11 @@
         P(("ctx", "head"), None),
         P("ctx"),
     )
+
+    def step(*args):
+        heads = args[2].shape[2] // HEAD_DIM
+        return (heads_body if 2 * heads == lax.axis_size("ctx") else body)(*args)
+
     return jax.shard_map(
-        body, mesh=mesh, in_specs=placed, out_specs=P(("ctx", "head"), None), check_vma=False
+        step, mesh=mesh, in_specs=placed, out_specs=P(("ctx", "head"), None), check_vma=False
     )

time: 252 us -> 258 us (1.024)
  the two profiles are of different devices: /device:TPU:11 before, /device:TPU:0 now
where the time goes in v1:
time: 258 us; the launch traced here: 259 us
  Pallas kernels  171 us (66%)
  waiting for transfers between devices  69.4 us (27%)
  between operations  13.4 us (5%)
  local copies, waits for them, and re-layouts  5.52 us (2%)
    pallas_call x1, Pallas kernels, finish_step(): pl.pallas_call(functools.partial(finish_kernel, ctx_count, head_count), o...  53.7 us
    pallas_call x1, Pallas kernels, project_heads(): pl.pallas_call(functools.partial(project_kernel, ctx_count, head_count),...  40.1 us
    all_gather x1, waiting for transfers between devices, heads_body(): lax.all_gather(lax.all_gather(w_part, 'head', axis=0), 'ctx', axis=0)  37 us
    pallas_call x1, Pallas kernels, readout_step(): pl.pallas_call(functools.partial(readout_kernel, ctx_count, head_count),...  34.7 us
    all_gather x1, waiting for transfers between devices, heads_body(): lax.all_gather(w_part, 'head', axis=0)  32.3 us
    pallas_call x1, Pallas kernels, heads_body(): pl.pallas_call(functools.partial(head_forward_kernel, rows, own, parts, s...  21.3 us
    pallas_call x1, Pallas kernels, heads_body(): pl.pallas_call(functools.partial(head_backward_kernel, rows, own, parts,...  21.1 us
  transfers between devices with their start and end apart: 2, of which 2 were waited for; matrix products, arithmetic and copies ran while one was open for 0% of the time, Pallas kernels for 24%

profile of v1, /device:TPU:0, one launch (start us, length us, event | category | flops | bytes accessed | tf_op | source)
XLA Modules:
  0.0 259.3 jit_solution(16163449215731757754)
XLA Ops:
  6.5 0.0 copy-start
  6.5 0.0 all-gather.5.cloned.1.call-start
  6.5 1.2 copy-done
  7.8 0.7 constant_dynamic-slice_fusion
  8.5 0.0 all-gather.5.cloned.1.call-update
  8.5 0.0 all-gather.7.cloned.1.call-start
  8.6 32.3 %all-gather.5.cloned.1.call-done = bf16[512,2048]{1,0:T(8,128)(2,1)} async-done(((bf16[64,2048]{1,0:T(8,128)(2,1)}), bf16[512,2048]{1,0:T(8,128)(2,1)}) %all-gather.5.cloned.1.call-update) | async-done | bytes 2097168 | tf_op jit(solution)/shard_map/all_gather | solution.py:1418
  40.8 0.0 all-gather.7.cloned.1.call-update
  40.9 1.3 reshape.24.gain_ref
  42.2 40.1 %shard_map.73 = (bf16[4,4,128,128]{3,2,1,0:T(8,128)(2,1)}, bf16[2,4,4,256,128]{4,3,2,1,0:T(8,128)(2,1)}, s32[4,8,128]{2,1,0:T(8,128)}) custom-call(bf16[1024,2048]{1,0:T(8,128)(2,1)} %state_any.5, bf16[3,2048,256]{2,1,0:T(8,128)(2,1)} %w_any.3, bf16[1,2048]{1,0:T(2,128)(2,1)} %reshape.24.gain_ref, s32[8,128]{1,0:T(8,128)} %bitcast.14), custom_call_target="tpu_custom_call" | custom-call | tf_op jit(solution)/shard_map/pallas_call | solution.py:841
  82.2 21.3 %shard_map.74 = (bf16[2048,128]{1,0:T(8,128)(2,1)}, f32[4,2,256]{2,1,0:T(2,128)}) custom-call(s32[4,8,128]{2,1,0:T(8,128)} %get-tuple-element.14.segs_ref, bf16[2048,128]{1,0:T(8,128)(2,1)} %bitcast.17, bf16[2,4096,128]{2,1,0:T(8,128)(2,1)} %bitcast.15), custom_call_target="tpu_custom_call" | custom-call | flops 4294967296 | tf_op jit(solution)/shard_map/pallas_call | solution.py:1426
  103.5 37.0 %all-gather.7.cloned.1.call-done = bf16[32,64,2048]{2,1,0:T(8,128)(2,1)} async-done(((bf16[8,64,2048]{2,1,0:T(8,128)(2,1)}), bf16[32,64,2048]{2,1,0:T(8,128)(2,1)}) %all-gather.7.cloned.1.call-update) | async-done | bytes 8388624 | tf_op jit(solution)/shard_map/all_gather | solution.py:1418
  140.6 34.7 %shard_map.75 = (bf16[4,4,128,128]{3,2,1,0:T(8,128)(2,1)}, f32[128,2048]{1,0:T(8,128)}) custom-call(bf16[4,4,128,128]{3,2,1,0:T(8,128)(2,1)} %bitcast.12, bf16[4,8,64,2048]{3,2,1,0:T(8,128)(2,1)} %bitcast.9, bf16[1024,2048]{1,0:T(8,128)(2,1)} %state_any.5, bf16[1024,2048]{1,0:T(8,128)(2,1)} %probe_any.1), custom_call_target="tpu_custom_call" | custom-call | tf_op jit(solution)/shard_map/pallas_call | solution.py:1178
  175.3 21.1 %shard_map.76 = (bf16[2048,128]{1,0:T(8,128)(2,1)}, bf16[4096,256]{1,0:T(8,128)(2,1)}) custom-call(s32[4,8,128]{2,1,0:T(8,128)} %get-tuple-element.14.segs_ref, bf16[2048,128]{1,0:T(8,128)(2,1)} %bitcast.18, bf16[2,4096,128]{2,1,0:T(8,128)(2,1)} %bitcast.16, bf16[2048,128]{1,0:T(8,128)(2,1)} %bitcast.19, bf16[2048,128]{1,0:T(8,128)(2,1)} %get-tuple-element.17.out_ref, ...), custom_call_target="tpu_custom_call" | custom-call | flops 10737418240 | tf_op jit(solution)/shard_map/pallas_call | solution.py:1443
  196.4 53.7 %shard_map.77 = f32[128,2048]{1,0:T(8,128)} custom-call(bf16[4,4,128,128]{3,2,1,0:T(8,128)(2,1)} %bitcast.13, bf16[4,4,2,128,256]{4,3,2,1,0:T(8,128)(2,1)} %bitcast.11, bf16[3,2048,256]{2,1,0:T(8,128)(2,1)} %w_any.3, bf16[1024,2048]{1,0:T(8,128)(2,1)} %state_any.5, bf16[128,2048]{1,0:T(8,128)(2,1)} %noise_ref.1, f32[128,2048]{1,0:T(8,128)} %get-tuple-element.22.readout_ref, ...), custom_call_target="tpu_custom_call" | custom-call | tf_op jit(solution)/shard_map/pallas_call | solution.py:1382
  250.2 2.3 copy.9
Async XLA Ops:
  6.5 1.2 copy-start
  6.5 34.3 %all-gather.5.cloned.1.call-start = ((), (), s32[]{:S(2)}) async-start(), calls=%async_computation | async-start | bytes 2359296 | tf_op jit(solution)/shard_map/all_gather | solution.py:1418
  8.5 132.1 %all-gather.7.cloned.1.call-start = ((), (), s32[]{:S(2)}) async-start(), calls=%async_computation.1 | async-start | bytes 10485760 | tf_op jit(solution)/shard_map/all_gather | solution.py:1418
Sparse Core Ops, SparseCore 0:
  8.9 31.8 all-gather.4
  42.7 97.8 all-gather.6

commit v2 on v1

--- a/solution.py
+++ b/solution.py
@@ -646,10 +646,13 @@
     return result
 
 
-def project_kernel(
-    ctx_count, head_count, state_any, w_any, gain_ref, seg_ref, query_out, kv_out, segs_out,
-    state_v, w_v, query_buf, kv_buf, state_sem, w_sem, q_send, q_recv, kv_send, kv_recv, pass_send,
-    seg_send, seg_recv, own_q, own_kv, own_seg,
+def front_kernel(
+    ctx_count, head_count, state_any, w_any, gain_ref, seg_ref, w_out_any, probe_any, query_out,
+    kv_out, segs_out, part_out, log_out, grad_out, readout_out, state_v, w_v, query_buf, kv_buf,
+    w_ref, joined, half, sending, state_own, probe_own, load_sem, w_sem, q_send, q_recv, kv_send,
+    kv_recv, pass_send, seg_send, seg_recv, own_q, own_kv, line_send, line_recv, plane_send,
+    plane_recv, beside_send, beside_recv, shard_send, shard_recv, shard_sem, out_send, out_recv,
+    back_send, back_recv, own_sem, row_sem,
 ):
     ctx, me, group, core = place()
     rows, model = state_any.shape
@@ -661,9 +664,12 @@
     def at(piece):
         return pl.ds(pl.multiple_of(piece * chunk, chunk), chunk)
 
+    def own_at(piece):
+        return pl.ds(pl.multiple_of(piece * own, own), own)
+
     def load_state(piece):
         return pltpu.make_async_copy(
-            state_any.at[at(piece)], state_v.at[at(piece)], state_sem.at[piece]
+            state_any.at[at(piece)], state_v.at[at(piece)], load_sem.at[piece]
         )
 
     load_state(0).start()
@@ -672,9 +678,129 @@
         copy.start()
     for piece in range(1, groups):
         load_state(piece).start()
-    peers = [(lax.rem(ctx + step, ctx_count), me) for step in range(1, ctx_count)]
-    peers += [(lax.rem(ctx + step, ctx_count), partner) for step in range(ctx_count)]
+    my_rows = own_at(me)
+    shard = w_out_any.shape[0]
+    part, quarter = shard // 2, shard // ctx_count
+    later_loads = [
+        pltpu.make_async_copy(state_any.at[my_rows], state_own, row_sem.at[0]),
+        pltpu.make_async_copy(probe_any.at[my_rows], probe_own, row_sem.at[1]),
+        pltpu.make_async_copy(
+            w_out_any, w_ref.at[pl.ds(pl.multiple_of(me * shard, shard), shard)], shard_sem
+        ),
+    ]
+    for copy in later_loads:
+        copy.start()
+    peers = [(lax.rem(ctx + step, ctx_count), partner) for step in range(ctx_count)]
+    for far in range(groups):
+        for step in range(ctx_count):
+            if far or step:
+                peers.append(
+                    (lax.rem(ctx + step, ctx_count), lax.rem(group + far, groups) * 2 + core)
+                )
     meet(peers)
+
+    low, high = lax.rem(ctx, 2), ctx // 2
+    which = lax.rem(low + high, 2)
+    across, along = high * 2 + 1 - low, (1 - high) * 2 + low
+
+    def shard_rows(origin, first, size):
+        return pl.ds(pl.multiple_of((origin * 2 + core) * shard + first, size), size)
+
+    def line_copy(way, origin, mine):
+        here = shard_rows(origin, which * part, part)
+        source = (
+            w_out_any.at[pl.ds(pl.multiple_of(which * part, part), part)]
+            if mine
+            else w_ref.at[here]
+        )
+        other = group + 1 if way == 0 else group - 1
+        return remote(
+            source, w_ref.at[here], line_send.at[way, origin], line_recv.at[origin], ctx,
+            other * 2 + core,
+        )
+
+    def plane_copy(axis, origin, kept):
+        here = shard_rows(origin, kept * part + axis * quarter, quarter)
+        return remote(
+            w_ref.at[here], w_ref.at[here], plane_send.at[axis, origin],
+            plane_recv.at[axis, origin], along if axis else across, me,
+        )
+
+    def beside_copy(kind, origin):
+        here = shard_rows(origin, jnp.where(kind == 0, which, 1 - which) * part, part)
+        return remote(
+            w_ref.at[here], w_ref.at[here], beside_send.at[kind, origin],
+            beside_recv.at[kind, origin], ctx, partner,
+        )
+
+    def shard_copy():
+        return remote(
+            w_out_any, w_ref.at[pl.ds(pl.multiple_of(me * shard, shard), shard)], shard_send,
+            shard_recv, ctx, partner,
+        )
+
+    has_up, has_down = group < groups - 1, group > 0
+
+    @pl.when(has_up)
+    def _():
+        line_copy(0, group, True).start()
+
+    @pl.when(has_down)
+    def _():
+        line_copy(1, group, True).start()
+
+    shard_copy().start()
+
+    def each_origin(distance, work):
+        for way in range(2):
+            origin = group - distance if way == 0 else group + distance
+
+            @pl.when(origin >= 0 if way == 0 else origin < groups)
+            def _():
+                work(way, origin)
+
+    def line_arrived(distance):
+        def work(way, origin):
+            line_copy(way, origin, False).wait_recv()
+
+            @pl.when(has_up if way == 0 else has_down)
+            def _():
+                line_copy(way, origin, False).start()
+
+            for axis in range(2):
+                plane_copy(axis, origin, which).start()
+            beside_copy(0, origin).start()
+
+        each_origin(distance, work)
+
+    def plane_arrived(distance):
+        def work(way, origin):
+            for axis in range(2):
+                plane_copy(axis, origin, 1 - which).wait_recv()
+            beside_copy(1, origin).start()
+
+        each_origin(distance, work)
+
+    def weights_sent(distance):
+        def work(way, origin):
+            @pl.when(has_up if way == 0 else has_down)
+            def _():
+                line_copy(way, origin, False).wait_send()
+
+            for axis in range(2):
+                plane_copy(axis, origin, which).wait_send()
+            for kind in range(2):
+                beside_copy(kind, origin).wait_send()
+
+        each_origin(distance, work)
+
+    def beside_arrived(distance):
+        def work(way, origin):
+            for kind in range(2):
+                beside_copy(kind, origin).wait_recv()
+
+        each_origin(distance, work)
+
     segs = []
     for step in range(1, ctx_count):
         copy = remote(
@@ -683,9 +809,7 @@
         )
         copy.start()
         segs.append(copy)
-    copy = pltpu.make_async_copy(seg_ref, segs_out.at[ctx], own_seg)
-    copy.start()
-    segs.append(copy)
+    segs_out[ctx] = seg_ref[...]
     for copy in w_loads:
         copy.wait()
     gain = gain_ref[...].astype(jnp.float32)
@@ -694,41 +818,26 @@
         head = group * 2 + kind
         return (
             remote(
-                query_buf.at[slot, piece, kind], query_out.at[ctx, piece],
+                query_buf.at[slot, piece, kind], query_out.at[ctx, own_at(piece)],
                 q_send.at[slot, kind, piece], q_recv.at[ctx, piece], dest, head,
             ),
             remote(
-                kv_buf.at[slot, kind, piece], kv_out.at[kind, ctx, piece],
+                kv_buf.at[slot, kind, piece], kv_out.at[kind, ctx, at(piece)],
                 kv_send.at[slot, kind, piece], kv_recv.at[kind, ctx, piece], dest, head,
             ),
         )
-
-    def local(slot, piece):
-        result = [
-            pltpu.make_async_copy(
-                query_buf.at[slot, piece, core], query_out.at[ctx, piece], own_q.at[piece]
-            )
-        ]
-        for kind in range(2):
-            result.append(
-                pltpu.make_async_copy(
-                    kv_buf.at[slot, kind, piece], kv_out.at[kind, ctx, piece],
-                    own_kv.at[kind, piece],
-                )
-            )
-        return result
 
     def beside(slot, piece):
         result = [
             remote(
-                query_buf.at[slot, piece, 1 - core], query_out.at[ctx, piece],
+                query_buf.at[slot, piece, 1 - core], query_out.at[ctx, own_at(piece)],
                 q_send.at[slot, 1 - core, piece], q_recv.at[ctx, piece], ctx, partner,
             )
         ]
         for kind in range(2):
             result.append(
                 remote(
-                    kv_buf.at[slot, kind, piece], kv_out.at[kind, ctx, piece],
+                    kv_buf.at[slot, kind, piece], kv_out.at[kind, ctx, at(piece)],
                     kv_send.at[slot, kind, piece], kv_recv.at[kind, ctx, piece], ctx, partner,
                 )
             )
@@ -743,12 +852,12 @@
                 jnp.bfloat16
             )
             for slot in range(slots):
-                part = result[:, slot * HEAD_DIM : (slot + 1) * HEAD_DIM]
+                cut = result[:, slot * HEAD_DIM : (slot + 1) * HEAD_DIM]
                 if t == 0:
-                    query_buf[slot, piece, 0] = part[:own]
-                    query_buf[slot, piece, 1] = part[own:]
+                    query_buf[slot, piece, 0] = cut[:own]
+                    query_buf[slot, piece, 1] = cut[own:]
                 else:
-                    kv_buf[slot, t - 1, piece] = part
+                    kv_buf[slot, t - 1, piece] = cut
         for slot in range(slots):
             dest = core * slots + slot
 
@@ -760,17 +869,21 @@
 
             @pl.when(dest == ctx)
             def _():
-                for copy in local(slot, piece) + beside(slot, piece):
+                for copy in beside(slot, piece):
                     copy.start()
+                query_out[ctx, own_at(piece), :] = query_buf[slot, piece, core]
+                for kind in range(2):
+                    kv_out[kind, ctx, at(piece), :] = kv_buf[slot, kind, piece]
 
         return 0
 
     lax.fori_loop(0, groups, project, 0)
+    line_arrived(1)
 
     def hand_over(piece, step):
         source = lax.rem(ctx + step, ctx_count)
         return remote(
-            kv_out.at[core, source, piece], kv_out.at[core, source, piece],
+            kv_out.at[core, source, at(piece)], kv_out.at[core, source, at(piece)],
             pass_send.at[step, piece], kv_recv.at[core, source, piece], ctx, partner,
         )
 
@@ -782,27 +895,188 @@
         return 0
 
     lax.fori_loop(0, groups, forward, 0)
+    line_arrived(2)
+    plane_arrived(1)
 
     def got_query(source, piece):
         remote(
-            query_out.at[source, piece], query_out.at[source, piece], q_send.at[0, 0, piece],
-            q_recv.at[source, piece], ctx, partner,
+            query_out.at[source, own_at(piece)], query_out.at[source, own_at(piece)],
+            q_send.at[0, 0, piece], q_recv.at[source, piece], ctx, partner,
         ).wait_recv()
 
     def got_kv(kind, source, piece):
         remote(
-            kv_out.at[kind, source, piece], kv_out.at[kind, source, piece],
+            kv_out.at[kind, source, at(piece)], kv_out.at[kind, source, at(piece)],
             kv_send.at[0, 0, piece], kv_recv.at[kind, source, piece], ctx, partner,
         ).wait_recv()
 
-    mine = ctx // slots == core
-
-    def finish(piece, _):
+    def gather(piece, _):
         for step in range(1, ctx_count):
             source = lax.rem(ctx + step, ctx_count)
             got_query(source, piece)
             got_kv(1 - core, source, piece)
             hand_over(piece, step).wait_send()
+
+        @pl.when(ctx // slots != core)
+        def _():
+            got_query(ctx, piece)
+            for kind in range(2):
+                got_kv(kind, ctx, piece)
+
+        return 0
+
+    lax.fori_loop(0, groups, gather, 0)
+    for copy in segs:
+        copy.wait()
+
+    def cols_of(group_at, ctx_at):
+        head = group_at * ctx_count + ctx_at
+        return pl.ds(pl.multiple_of(head * HEAD_DIM, HEAD_DIM), HEAD_DIM)
+
+    factor = HEAD_DIM ** (-0.5) * LOG2E
+    sub = groups * own
+    seg_all = segs_out[...]
+
+    def below(value):
+        count = jnp.where(seg_all < value, 1.0, 0.0)
+        for axis in (0, 1, 2):
+            count = jnp.sum(count, axis=axis, keepdims=True)
+        return count[0]
+
+    first_bound, second_bound = below(1), below(2)
+    lane = lax.broadcasted_iota(jnp.int32, (1, sub), 1)
+    inside = (lane // own) * (2 * own) + core * own + lane % own
+    key_row = lax.broadcasted_iota(jnp.int32, (rows, sub), 0)
+
+    def out_copy(tile, order, other):
+        return remote(
+            part_out.at[tile, own_at(other)], joined.at[:, cols_of(group, ctx)],
+            out_send.at[tile, order], out_recv.at[group, ctx], tile, other * 2 + core,
+        )
+
+    def one_tile(tile, _):
+        query = query_out[tile]
+        pos = (tile * rows + inside).astype(jnp.float32)
+        start = jnp.where(
+            pos >= second_bound, second_bound, jnp.where(pos >= first_bound, first_bound, 0.0)
+        ).astype(jnp.int32)
+
+        def step(diagonal, piece, carry):
+            top, total, acc = carry
+            scores = dot32(kv_out[0, piece], query, NT)
+            allowed = key_row >= start - piece * rows
+            if diagonal:
+                allowed = allowed & (key_row <= inside)
+            scores = jnp.where(allowed, scores, NEGATIVE)
+            new_top = jnp.maximum(top, jnp.max(scores, axis=0, keepdims=True) * factor)
+            weights = jnp.exp2(scores * factor - new_top)
+            scale = jnp.exp2(top - new_top)
+            total = total * scale + jnp.sum(weights, axis=0, keepdims=True)
+            acc = acc * scale + dot32(kv_out[1, piece], weights.astype(jnp.bfloat16), TN)
+            return new_top, total, acc
+
+        carry = (
+            jnp.full((1, sub), NEGATIVE, jnp.float32),
+            jnp.zeros((1, sub), jnp.float32),
+            jnp.zeros((HEAD_DIM, sub), jnp.float32),
+        )
+        carry = lax.fori_loop(0, tile, functools.partial(step, False), carry)
+        top, total, acc = step(True, tile, carry)
+        part_out[tile] = (acc / total).T.astype(jnp.bfloat16)
+        log_out[tile] = top + jnp.log2(total)
+        for order in range(groups):
+            other = far_first(groups, group, order)
+            if order == groups - 1:
+
+                @pl.when(tile != ctx)
+                def _():
+                    out_copy(tile, order, other).start()
+
+                @pl.when(tile == ctx)
+                def _():
+                    joined[:, cols_of(group, ctx)] = part_out[tile, own_at(group), :]
+
+            else:
+                out_copy(tile, order, other).start()
+
+        for distance in range(3, groups):
+
+            @pl.when(tile == distance - 1)
+            def _():
+                line_arrived(distance)
+                plane_arrived(distance - 1)
+
+        return 0
+
+    lax.fori_loop(0, ctx_count, one_tile, 0)
+    for distance in range(max(2, groups - 1), groups):
+        plane_arrived(distance)
+    for copy in later_loads:
+        copy.wait()
+    sources = []
+    for far in range(groups):
+        for step in range(ctx_count):
+            if far or step:
+                sources.append((lax.rem(group + far, groups), lax.rem(ctx + step, ctx_count)))
+    for other, peer in sources:
+        remote(
+            part_out.at[0, own_at(0)], joined.at[:, cols_of(other, peer)], out_send.at[0, 0],
+            out_recv.at[other, peer], peer, other * 2 + core,
+        ).wait_recv()
+    shard_copy().wait_recv()
+    for distance in range(1, groups):
+        beside_arrived(distance)
+    tile = min(256, model)
+
+    def layer(piece, carry):
+        squares, products = carry
+        cols = pl.ds(pl.multiple_of(piece * tile, tile), tile)
+        layer = state_own[:, cols].astype(jnp.float32) + jnp.dot(
+            joined[...], w_ref[:, cols], preferred_element_type=jnp.float32
+        )
+        readout_out[:, cols] = layer
+        squares = squares + jnp.sum(layer * layer, axis=1, keepdims=True)
+        products = products + jnp.sum(
+            layer * probe_own[:, cols].astype(jnp.float32), axis=1, keepdims=True
+        )
+        return squares, products
+
+    zero = jnp.zeros((own, 1), jnp.float32)
+    squares, products = lax.fori_loop(0, model // tile, layer, (zero, zero))
+    scale = lax.rsqrt(squares / model + EPSILON)
+    bend = scale**3 * (products / model)
+
+    def finish(piece, _):
+        cols = pl.ds(pl.multiple_of(piece * tile, tile), tile)
+        readout = scale * probe_own[:, cols].astype(jnp.float32) - readout_out[:, cols] * bend
+        readout_out[:, cols] = readout
+        half[:, cols] = readout.astype(jnp.bfloat16)
+        return 0
+
+    lax.fori_loop(0, model // tile, finish, 0)
+    wide = ctx_count * HEAD_DIM
+    copies = []
+    for order in range(groups):
+        other = far_first(groups, group, order)
+        result = dot32(
+            half[...], w_ref[pl.ds(pl.multiple_of(other * wide, wide), wide), :], NT
+        ).astype(jnp.bfloat16)
+        for index in range(ctx_count):
+            sending[order, index] = result[:, index * HEAD_DIM : (index + 1) * HEAD_DIM]
+        for step in range(ctx_count):
+            peer = lax.rem(ctx + step, ctx_count)
+            if order == groups - 1 and step == 0:
+                continue
+            copy = remote(
+                sending.at[order, peer], grad_out.at[ctx, group], back_send.at[order, step],
+                back_recv.at[ctx, group], peer, other * 2 + core,
+            )
+            copy.start()
+            copies.append(copy)
+    last = pltpu.make_async_copy(sending.at[groups - 1, ctx], grad_out.at[ctx, group], own_sem)
+    last.start()
+
+    def sent(piece, _):
         for slot in range(slots):
             dest = core * slots + slot
 
@@ -814,44 +1088,80 @@
 
             @pl.when(dest == ctx)
             def _():
-                for copy in local(slot, piece):
-                    copy.wait()
                 for copy in beside(slot, piece):
                     copy.wait_send()
 
-        @pl.when(jnp.logical_not(mine))
-        def _():
-            got_query(ctx, piece)
-            for kind in range(2):
-                got_kv(kind, ctx, piece)
-
-        return 0
-
-    lax.fori_loop(0, groups, finish, 0)
-    for copy in segs:
-        copy.wait()
-
-
-def project_heads(ctx_count, head_count, state, w_qkv, gain, segment_ids):
+        return 0
+
+    lax.fori_loop(0, groups, sent, 0)
+
+    @pl.when(has_up)
+    def _():
+        line_copy(0, group, True).wait_send()
+
+    @pl.when(has_down)
+    def _():
+        line_copy(1, group, True).wait_send()
+
+    shard_copy().wait_send()
+    for distance in range(1, groups):
+        weights_sent(distance)
+
+    def parts_sent(tile, _):
+        for order in range(groups):
+            other = far_first(groups, group, order)
+            if order == groups - 1:
+
+                @pl.when(tile != ctx)
+                def _():
+                    out_copy(tile, order, other).wait_send()
+
+            else:
+                out_copy(tile, order, other).wait_send()
+        return 0
+
+    lax.fori_loop(0, ctx_count, parts_sent, 0)
+    for other, peer in sources:
+        remote(
+            sending.at[0, 0], grad_out.at[peer, other], back_send.at[0, 0],
+            back_recv.at[peer, other], peer, other * 2 + core,
+        ).wait_recv()
+    for copy in copies:
+        copy.wait_send()
+    last.wait()
+
+
+def front(ctx_count, head_count, state, w_qkv, gain, segment_ids, w_out, probe):
     rows, model = state.shape
     width = w_qkv.shape[2]
     own, groups, slots = rows // head_count, head_count // 2, width // HEAD_DIM
     seg = segment_ids.reshape(-1, 128)
-    half, dma = jnp.bfloat16, pltpu.SemaphoreType.DMA
+    half, full, dma = jnp.bfloat16, jnp.float32, pltpu.SemaphoreType.DMA
+    shape = jax.ShapeDtypeStruct
     return pl.pallas_call(
-        functools.partial(project_kernel, ctx_count, head_count),
+        functools.partial(front_kernel, ctx_count, head_count),
         out_shape=(
-            jax.ShapeDtypeStruct((ctx_count, groups, own, HEAD_DIM), half),
-            jax.ShapeDtypeStruct((2, ctx_count, groups, 2 * own, HEAD_DIM), half),
-            jax.ShapeDtypeStruct((ctx_count,) + seg.shape, seg.dtype),
+            shape((ctx_count, groups * own, HEAD_DIM), half),
+            shape((2, ctx_count, rows, HEAD_DIM), half),
+            shape((ctx_count,) + seg.shape, seg.dtype),
+            shape((ctx_count, groups * own, HEAD_DIM), half),
+            shape((ctx_count, 1, groups * own), full),
+            shape((ctx_count, groups, own, HEAD_DIM), half),
+            shape((own, model), full),
         ),
-        in_specs=[ANY, ANY, VMEM, VMEM],
-        out_specs=(ANY, ANY, ANY),
+        in_specs=[ANY, ANY, VMEM, VMEM, ANY, ANY],
+        out_specs=(VMEM, VMEM, VMEM, VMEM, VMEM, ANY, VMEM),
         scratch_shapes=[
             pltpu.VMEM((rows, model), half),
             pltpu.VMEM(w_qkv.shape, half),
             pltpu.VMEM((slots, groups, 2, own, HEAD_DIM), half),
             pltpu.VMEM((slots, 2, groups, 2 * own, HEAD_DIM), half),
+            pltpu.VMEM((model, model), half),
+            pltpu.VMEM((own, model), half),
+            pltpu.VMEM((own, model), half),
+            pltpu.VMEM((groups, ctx_count, own, HEAD_DIM), half),
+            pltpu.VMEM((own, model), half),
+            pltpu.VMEM((own, model), half),
             dma((groups,)),
             dma((3,)),
             dma((slots, 2, groups)),
@@ -863,12 +1173,26 @@
             dma((ctx_count,)),
             dma((groups,)),
             dma((2, groups)),
+            dma((2, groups)),
+            dma((groups,)),
+            dma((2, groups)),
+            dma((2, groups)),
+            dma((2, groups)),
+            dma((2, groups)),
             dma,
+            dma,
+            dma,
+            dma((ctx_count, groups)),
+            dma((groups, ctx_count)),
+            dma((groups, ctx_count)),
+            dma((ctx_count, groups)),
+            dma,
+            dma((2,)),
         ],
         compiler_params=pltpu.CompilerParams(
-            collective_id=0, has_side_effects=True, vmem_limit_bytes=60 * 2**20
+            collective_id=0, has_side_effects=True, vmem_limit_bytes=62 * 2**20
         ),
-    )(state, w_qkv, gain, seg)
+    )(state, w_qkv, gain, seg, w_out, probe)
 
 
 def segment_bounds(segs_ref):
@@ -899,61 +1223,6 @@
     inner_high = jnp.maximum(inner_low, (first + 1) // bk)
     high = last // bk + 1
     return places, low, inner_low, inner_high, high
-
-
-def head_forward_kernel(
-    rows, own, parts, sub, bk, segs_ref, query_ref, kv_ref, out_ref, log_ref
-):
-    factor = HEAD_DIM ** (-0.5) * LOG2E
-    core = lax.rem(lax.axis_index("head"), 2)
-    bounds = segment_bounds(segs_ref)
-    tiles = query_ref.shape[0] // (parts * sub)
-
-    def one_tile(tile, _):
-        places, low, inner_low, inner_high, high = tile_plan(
-            bounds, rows, own, parts, sub, bk, tile, core
-        )
-
-        def at(part):
-            return pl.ds(pl.multiple_of((tile * parts + part) * sub, sub), sub)
-
-        def step(masked, piece, carry):
-            keys_at = pl.ds(pl.multiple_of(piece * bk, bk), bk)
-            if masked:
-                key_pos = piece * bk + lax.broadcasted_iota(jnp.int32, (bk, sub), 0)
-            result = []
-            for part in range(parts):
-                top, total, acc = carry[part]
-                scores = dot32(kv_ref[0, keys_at, :], query_ref[at(part), :], NT)
-                if masked:
-                    start, pos = places[part]
-                    scores = jnp.where((key_pos >= start) & (key_pos <= pos), scores, NEGATIVE)
-                new_top = jnp.maximum(top, jnp.max(scores, axis=0, keepdims=True) * factor)
-                weights = jnp.exp2(scores * factor - new_top)
-                scale = jnp.exp2(top - new_top)
-                total = total * scale + jnp.sum(weights, axis=0, keepdims=True)
-                acc = acc * scale + dot32(kv_ref[1, keys_at, :], weights.astype(jnp.bfloat16), TN)
-                result.append((new_top, total, acc))
-            return tuple(result)
-
-        carry = tuple(
-            (
-                jnp.full((1, sub), NEGATIVE, jnp.float32),
-                jnp.zeros((1, sub), jnp.float32),
-                jnp.zeros((HEAD_DIM, sub), jnp.float32),
-            )
-            for _ in range(parts)
-        )
-        carry = lax.fori_loop(low, inner_low, functools.partial(step, True), carry)
-        carry = lax.fori_loop(inner_low, inner_high, functools.partial(step, False), carry)
-        carry = lax.fori_loop(inner_high, high, functools.partial(step, True), carry)
-        for part in range(parts):
-            top, total, acc = carry[part]
-            out_ref[at(part), :] = (acc / total).T.astype(jnp.bfloat16)
-            log_ref[tile, pl.ds(part, 1), :] = top + jnp.log2(total)
-        return 0
-
-    lax.fori_loop(0, tiles, one_tile, 0)
 
 
 def head_backward_kernel(
@@ -1035,173 +1304,6 @@
         return 0
 
     lax.fori_loop(0, pair_rows // bk, flush, 0)
-
-
-def readout_kernel(
-    ctx_count, head_count, part_ref, w_any, state_any, probe_any, grad_out, readout_out, w_ref,
-    joined, half, sending, state_own, probe_own, out_send, out_recv, back_send, back_recv, own_sem,
-    w_sem, row_sem,
-):
-    ctx, me, group, core = place()
-    groups = head_count // 2
-    own, model = readout_out.shape
-    my_rows = pl.ds(pl.multiple_of(me * own, own), own)
-    row_loads = [
-        pltpu.make_async_copy(state_any.at[my_rows], state_own, row_sem.at[0]),
-        pltpu.make_async_copy(probe_any.at[my_rows], probe_own, row_sem.at[1]),
-    ]
-    for copy in row_loads:
-        copy.start()
-    quarter = w_any.shape[2]
-
-    def load_w(index):
-        piece, head = index // head_count, lax.rem(index, head_count)
-        first = pl.multiple_of((head * ctx_count + piece) * quarter, quarter)
-        return pltpu.make_async_copy(
-            w_any.at[piece, head], w_ref.at[pl.ds(first, quarter)], w_sem.at[index]
-        )
-
-    def start_w(index, _):
-        load_w(index).start()
-        return 0
-
-    def wait_w(index, _):
-        load_w(index).wait()
-        return 0
-
-    lax.fori_loop(0, ctx_count * head_count, start_w, 0)
-    peers = []
-    for far in range(groups):
-        for step in range(ctx_count):
-            if far or step:
-                peers.append(
-                    (lax.rem(ctx + step, ctx_count), lax.rem(group + far, groups) * 2 + core)
-                )
-    meet(peers)
-
-    def cols_of(group_at, ctx_at):
-        head = group_at * ctx_count + ctx_at
-        return pl.ds(pl.multiple_of(head * HEAD_DIM, HEAD_DIM), HEAD_DIM)
-
-    copies = []
-    for order in range(groups):
-        other = far_first(groups, group, order)
-        for step in range(ctx_count):
-            peer = lax.rem(ctx + step, ctx_count)
-            if order == groups - 1 and step == 0:
-                continue
-            copy = remote(
-                part_ref.at[peer, other], joined.at[:, cols_of(group, ctx)],
-                out_send.at[order, step], out_recv.at[group, ctx], peer, other * 2 + core,
-            )
-            copy.start()
-            copies.append(copy)
-    joined[:, cols_of(group, ctx)] = part_ref[ctx, group]
-    for copy in row_loads:
-        copy.wait()
-    lax.fori_loop(0, ctx_count * head_count, wait_w, 0)
-    sources = []
-    for far in range(groups):
-        for step in range(ctx_count):
-            if far or step:
-                sources.append((lax.rem(group + far, groups), lax.rem(ctx + step, ctx_count)))
-    for other, peer in sources:
-        remote(
-            part_ref.at[peer, other], joined.at[:, cols_of(other, peer)], out_send.at[0, 0],
-            out_recv.at[other, peer], peer, other * 2 + core,
-        ).wait_recv()
-    for copy in copies:
-        copy.wait_send()
-    tile = min(256, model)
-
-    def project(piece, carry):
-        squares, products = carry
-        cols = pl.ds(pl.multiple_of(piece * tile, tile), tile)
-        layer = state_own[:, cols].astype(jnp.float32) + jnp.dot(
-            joined[...], w_ref[:, cols], preferred_element_type=jnp.float32
-        )
-        readout_out[:, cols] = layer
-        squares = squares + jnp.sum(layer * layer, axis=1, keepdims=True)
-        products = products + jnp.sum(
-            layer * probe_own[:, cols].astype(jnp.float32), axis=1, keepdims=True
-        )
-        return squares, products
-
-    zero = jnp.zeros((own, 1), jnp.float32)
-    squares, products = lax.fori_loop(0, model // tile, project, (zero, zero))
-    scale = lax.rsqrt(squares / model + EPSILON)
-    bend = scale**3 * (products / model)
-
-    def finish(piece, _):
-        cols = pl.ds(pl.multiple_of(piece * tile, tile), tile)
-        readout = scale * probe_own[:, cols].astype(jnp.float32) - readout_out[:, cols] * bend
-        readout_out[:, cols] = readout
-        half[:, cols] = readout.astype(jnp.bfloat16)
-        return 0
-
-    lax.fori_loop(0, model // tile, finish, 0)
-    wide = ctx_count * HEAD_DIM
-    copies = []
-    for order in range(groups):
-        other = far_first(groups, group, order)
-        result = dot32(
-            half[...], w_ref[pl.ds(pl.multiple_of(other * wide, wide), wide), :], NT
-        ).astype(jnp.bfloat16)
-        for index in range(ctx_count):
-            sending[order, index] = result[:, index * HEAD_DIM : (index + 1) * HEAD_DIM]
-        for step in range(ctx_count):
-            peer = lax.rem(ctx + step, ctx_count)
-            if order == groups - 1 and step == 0:
-                continue
-            copy = remote(
-                sending.at[order, peer], grad_out.at[ctx, group], back_send.at[order, step],
-                back_recv.at[ctx, group], peer, other * 2 + core,
-            )
-            copy.start()
-            copies.append(copy)
-    copy = pltpu.make_async_copy(sending.at[groups - 1, ctx], grad_out.at[ctx, group], own_sem)
-    copy.start()
-    for other, peer in sources:
-        remote(
-            sending.at[0, 0], grad_out.at[peer, other], back_send.at[0, 0],
-            back_recv.at[peer, other], peer, other * 2 + core,
-        ).wait_recv()
-    for remote_copy in copies:
-        remote_copy.wait_send()
-    copy.wait()
-
-
-def readout_step(ctx_count, head_count, part, w_full, state, probe):
-    rows, model = state.shape
-    own, groups = rows // head_count, head_count // 2
-    half, full, dma = jnp.bfloat16, jnp.float32, pltpu.SemaphoreType.DMA
-    return pl.pallas_call(
-        functools.partial(readout_kernel, ctx_count, head_count),
-        out_shape=(
-            jax.ShapeDtypeStruct(part.shape, half),
-            jax.ShapeDtypeStruct((own, model), full),
-        ),
-        in_specs=[VMEM, ANY, ANY, ANY],
-        out_specs=(ANY, VMEM),
-        scratch_shapes=[
-            pltpu.VMEM((model, model), half),
-            pltpu.VMEM((own, model), half),
-            pltpu.VMEM((own, model), half),
-            pltpu.VMEM((groups, ctx_count, own, HEAD_DIM), half),
-            pltpu.VMEM((own, model), half),
-            pltpu.VMEM((own, model), half),
-            dma((groups, ctx_count)),
-            dma((groups, ctx_count)),
-            dma((groups, ctx_count)),
-            dma((ctx_count, groups)),
-            dma,
-            dma((ctx_count * head_count,)),
-            dma((2,)),
-        ],
-        compiler_params=pltpu.CompilerParams(
-            collective_id=1, has_side_effects=True, vmem_limit_bytes=60 * 2**20
-        ),
-    )(part, w_full, state, probe)
 
 
 def finish_kernel(
@@ -1413,33 +1515,12 @@
     rows, model = state.shape
     head_count, ctx_count = lax.axis_size("head"), lax.axis_size("ctx")
     own, groups = rows // head_count, head_count // 2
-    quarter = w_out.shape[0] // ctx_count
-    w_part = lax.dynamic_slice_in_dim(w_out, lax.axis_index("ctx") * quarter, quarter, 0)
-    w_full = lax.all_gather(lax.all_gather(w_part, "head", axis=0), "ctx", axis=0)
     gain = norm_gain.reshape(1, model)
-    queries, kv, segs = project_heads(ctx_count, head_count, state, w_qkv, gain, segment_ids)
+    queries, kv, segs, outputs, logs, grads_out, readout = front(
+        ctx_count, head_count, state, w_qkv, gain, segment_ids, w_out, probe
+    )
     mine, total = ctx_count * groups * own, ctx_count * rows
-    queries, kv = queries.reshape(mine, HEAD_DIM), kv.reshape(2, total, HEAD_DIM)
-    parts, sub = 2, groups * own // 2
-    tiles, bk = ctx_count, min(rows, 512)
-    params = pltpu.CompilerParams(vmem_limit_bytes=60 * 2**20)
-    outputs, logs = pl.pallas_call(
-        functools.partial(head_forward_kernel, rows, own, parts, sub, bk),
-        out_shape=(
-            jax.ShapeDtypeStruct((mine, HEAD_DIM), jnp.bfloat16),
-            jax.ShapeDtypeStruct((tiles, parts, sub), jnp.float32),
-        ),
-        in_specs=[VMEM] * 3,
-        out_specs=(VMEM, VMEM),
-        compiler_params=params,
-        cost_estimate=pl.CostEstimate(
-            flops=4 * mine * total * HEAD_DIM, bytes_accessed=0, transcendentals=0
-        ),
-    )(segs, queries, kv)
-    shape = (ctx_count, groups, own, HEAD_DIM)
-    grads_out, readout = readout_step(
-        ctx_count, head_count, outputs.reshape(shape), w_full, state, probe
-    )
+    parts, sub, bk = 1, groups * own, min(rows, 512)
     query_grad, pair = pl.pallas_call(
         functools.partial(head_backward_kernel, rows, own, parts, sub, bk),
         out_shape=(
@@ -1449,13 +1530,16 @@
         in_specs=[VMEM] * 6,
         out_specs=(VMEM, VMEM),
         scratch_shapes=[pltpu.VMEM((total, 2 * HEAD_DIM), jnp.float32)],
-        compiler_params=params,
+        compiler_params=pltpu.CompilerParams(vmem_limit_bytes=60 * 2**20),
         cost_estimate=pl.CostEstimate(
             flops=10 * mine * total * HEAD_DIM, bytes_accessed=0, transcendentals=0
         ),
-    )(segs, queries, kv, grads_out.reshape(mine, HEAD_DIM), outputs, logs)
+    )(
+        segs, queries.reshape(mine, HEAD_DIM), kv.reshape(2, total, HEAD_DIM),
+        grads_out.reshape(mine, HEAD_DIM), outputs.reshape(mine, HEAD_DIM), logs,
+    )
     return finish_step(
-        ctx_count, head_count, query_grad.reshape(shape),
+        ctx_count, head_count, query_grad.reshape(ctx_count, groups, own, HEAD_DIM),
         pair.reshape(ctx_count, groups, 2, own, 2 * HEAD_DIM), w_qkv, state, noise, readout, gain,
     )
 
@@ -1473,7 +1557,7 @@
 
     def step(*args):
         heads = args[2].shape[2] // HEAD_DIM
-        return (heads_body if 2 * heads == lax.axis_size("ctx") else body)(*args)
+        return (heads_body if lax.axis_size("ctx") == 2 * heads == 4 else body)(*args)
 
     return jax.shard_map(
         step, mesh=mesh, in_specs=placed, out_specs=P(("ctx", "head"), None), check_vma=False

time: 258 us -> 156 us (0.60)
  waiting for transfers between devices: 69.4 us -> 0 us
  Pallas kernels: 171 us -> 152 us
  between operations: 13.4 us -> 0.02 us
    all_gather x2 -> x0, waiting for transfers between devices: 69.3 us -> none  [the longest x1 37 us: heads_body(): lax.all_gather(lax.all_gather(w_part, 'head', axis=0), 'ctx', axis=0)]
    pallas_call x3 -> x1, Pallas kernels: 96.1 us -> 80.7 us  [front(): pl.pallas_call(functools.partial(front_kernel, ctx_count, head_count), ou...]
    pallas_call x1, Pallas kernels: 21.1 us -> 17.7 us  [heads_body(): pl.pallas_call(functools.partial(head_backward_kernel, rows, own, parts,...]
  transfers between devices with their start and end apart: 2 -> 0, of which waited for: 2 -> 0; matrix products, arithmetic and copies ran while one was open for 0% -> 0% of each run, Pallas kernels for 24% -> 0%
where the time goes in v2:
time: 156 us
  Pallas kernels  152 us (97%)
  local copies, waits for them, and re-layouts  3.58 us (2%)
    pallas_call x1, Pallas kernels, front(): pl.pallas_call(functools.partial(front_kernel, ctx_count, head_count), ou...  80.7 us
    pallas_call x1, Pallas kernels, finish_step(): pl.pallas_call(functools.partial(finish_kernel, ctx_count, head_count), o...  53.9 us
    pallas_call x1, Pallas kernels, heads_body(): pl.pallas_call(functools.partial(head_backward_kernel, rows, own, parts,...  17.7 us

profile of v2, /device:TPU:0, one launch (start us, length us, event | category | flops | bytes accessed | tf_op | source)
XLA Modules:
  0.0 155.9 jit_solution(17392090745755625440)
XLA Ops:
  0.0 1.3 reshape.24.gain_ref
  1.3 80.7 %shard_map.73 = (bf16[4,512,128]{2,1,0:T(8,128)(2,1)}, bf16[2,4,1024,128]{3,2,1,0:T(8,128)(2,1)}, s32[4,8,128]{2,1,0:T(8,128)}, bf16[4,512,128]{2,1,0:T(8,128)(2...) custom-call(bf16[1024,2048]{1,0:T(8,128)(2,1)} %state_any.3, ...), custom_call_target="tpu_custom_call" | custom-call | tf_op jit(solution)/shard_map/pallas_call | solution.py:1141
  82.0 17.7 %shard_map.74 = (bf16[2048,128]{1,0:T(8,128)(2,1)}, bf16[4096,256]{1,0:T(8,128)(2,1)}) custom-call(s32[4,8,128]{2,1,0:T(8,128)} %get-tuple-element.14.segs_ref, bf16[2048,128]{1,0:T(8,128)(2,1)} %bitcast.11, bf16[2,4096,128]{2,1,0:T(8,128)(2,1)} %bitcast.10, bf16[2048,128]{1,0:T(8,128)(2,1)} %bitcast.13, bf16[2048,128]{1,0:T(8,128)(2,1)} %bitcast.12, ...), custom_call_target="tpu_custom_call" | custom-call | flops 10737418240 | tf_op jit(solution)/shard_map/pallas_call | solution.py:1524
  99.7 53.9 %shard_map.75 = f32[128,2048]{1,0:T(8,128)} custom-call(bf16[4,4,128,128]{3,2,1,0:T(8,128)(2,1)} %bitcast.8, bf16[4,4,2,128,256]{4,3,2,1,0:T(8,128)(2,1)} %bitcast.7, bf16[3,2048,256]{2,1,0:T(8,128)(2,1)} %w_any.3, bf16[1024,2048]{1,0:T(8,128)(2,1)} %state_any.3, bf16[128,2048]{1,0:T(8,128)(2,1)} %noise_ref.1, f32[128,2048]{1,0:T(8,128)} %get-tuple-element.22.readout_ref, ...), custom_call_target="tpu_custom_call" | custom-call | tf_op jit(solution)/shard_map/pallas_call | solution.py:1484
  153.6 2.3 %copy.9 = f32[128,2048]{1,0:T(8,128)} copy(f32[128,2048]{1,0:T(8,128)} %shard_map.75) | data formatting | bytes 2097152
